TPU v7x, 512 devices: a whole 4x8x8 slice. The times are simulated.
512 devices in a mesh: gx: 4 (over x), gy: 8 (over y), gz: 16 (over z, core).
Axes of the slice: x: 4, y: 8, z: 8, core: 2. Of those that a mesh axis runs over, the one named last changes fastest.
Arguments:
- right_side: float32 [32, 128, 2048], P('gx', 'gy', 'gz'), may hold values from -6 to 6
- conductance: float32 [32, 128, 2048], P('gx', 'gy', 'gz'), may hold values from 0.25 to 4
- extents: int32 [4, 8, 16], P('gx', 'gy', 'gz'), may hold values from 64 to 128, as said below
- coarse_factor: bfloat16 [512, 512], replicated, may hold values from -1 to 3, as said below
Outputs:
- solution_field: float32 [32, 128, 2048], P('gx', 'gy', 'gz')
- residual: float32 [32, 128, 2048], P('gx', 'gy', 'gz')
Inputs may be any that keep to these rules, and one draw needn't show every extreme that they name: `extents`: cells of a block whose third local index is below its count are fluid, the others padding; in every draw some block has all 128 layers fluid. `coarse_factor`: lower triangular with a positive diagonal.
All inputs are finite; a program needn't handle non-finite values.
Results may differ from a plain program's by a relative error of at most 0.0003.
Values sent between devices are 32-bit elements; how exact they have to be, the bound alone decides.
A program may use at most 64 MiB of HBM per device.

v0:
```python
import jax
import jax.numpy as jnp
from jax import lax
from jax.sharding import Mesh
from jax.sharding import PartitionSpec as P

ITERS = 2
GZ = ("gz_0", "gz_1")


OMEGA = 0.8


def with_halo(x, sides, width):
    edges = {}
    for axis, dim in sides:
        size, length = (lax.axis_size(axis), x.shape[dim])
        up = [(i, (i + 1) % size) for i in range(size - 1)]
        last = lax.slice_in_dim(x, length - width, length, axis=dim)
        initial = lax.slice_in_dim(x, 0, width, axis=dim)
        edges[dim] = (
            lax.ppermute(last, axis, up),
            lax.ppermute(initial, axis, [(b, a) for a, b in up]),
        )
    done = []
    for _, dim in sides:
        low, high = edges[dim]
        around = [(width, width) if d in done else (0, 0) for d in range(x.ndim)]
        x = jnp.concatenate([jnp.pad(low, around), x, jnp.pad(high, around)], axis=dim)
        done.append(dim)
    return x


def from_everyone(x, axis):
    copies = jnp.broadcast_to(x, (lax.axis_size(axis), *x.shape))
    return lax.all_to_all(copies, axis, split_axis=0, concat_axis=0, tiled=True)


def laid_out(parts, dim):
    lengths = list(parts.shape[1:])
    lengths[dim] *= parts.shape[0]
    return jnp.moveaxis(parts, 0, dim).reshape(lengths)


def gathered_by_axis(x, axes, dim):
    far, near = axes
    initial = from_everyone(x, far)
    parts = jnp.swapaxes(from_everyone(initial, near), 0, 1)
    return laid_out(parts.reshape(-1, *x.shape), dim)


def taken_together(x, axis):
    everything = from_everyone(x, axis)
    return jnp.sum(everything, axis=0)


def by_axis(x, axes):
    far, near = axes
    nearer = taken_together(x, near)
    return taken_together(nearer, far)


def neighbour_slices():
    inner = slice(1, -1)
    return [
        (slice(2, None), inner, inner),
        (slice(None, -2), inner, inner),
        (inner, slice(2, None), inner),
        (inner, slice(None, -2), inner),
        (inner, inner, slice(2, None)),
        (inner, inner, slice(None, -2)),
    ]


def face_terms(padded, cond_padded):
    centre = (slice(1, -1), slice(1, -1), slice(1, -1))
    value_mid = padded[centre]
    cond_mid = cond_padded[centre]
    summed = jnp.zeros_like(value_mid)
    for place in neighbour_slices():
        summed = summed + 0.5 * (cond_mid + cond_padded[place]) * (value_mid - padded[place])
    return summed


def coef_total(cond_padded):
    centre = (slice(1, -1), slice(1, -1), slice(1, -1))
    cond_mid = cond_padded[centre]
    summed = jnp.zeros_like(cond_mid)
    for place in neighbour_slices():
        summed = summed + 0.5 * (cond_mid + cond_padded[place])
    return summed


def pool_sum(field):
    first, second, third = field.shape
    return field.reshape(first // 2, 2, second // 2, 2, third // 2, 2).sum(axis=(1, 3, 5))


def pool_max(field):
    first, second, third = field.shape
    return field.reshape(first // 2, 2, second // 2, 2, third // 2, 2).max(axis=(1, 3, 5))


def expand(field):
    first, second, third = field.shape
    wide = jnp.broadcast_to(field[:, None, :, None, :, None], (first, 2, second, 2, third, 2))
    return wide.reshape(2 * first, 2 * second, 2 * third)


def make_level(cond_padded, fluid, scale):
    inverse = fluid / (scale * coef_total(cond_padded) + 1.0 - fluid)
    return (cond_padded, fluid, scale, inverse)


def apply_level(field, level):
    padded = with_halo(field, (("gx", 0), ("gy", 1), (GZ, 2)), 1)
    return level[2] * level[1] * face_terms(padded, level[0])


def cycle(resid, levels):
    fine = levels[0]
    coarse_level = levels[1]
    first = OMEGA * fine[3] * resid
    image = apply_level(first, fine)
    below = OMEGA * coarse_level[3] * pool_sum(resid - image)
    return first + fine[1] * expand(below)


def on_device(right_side, conductance, extents, coarse_factor):
    factor = coarse_factor.astype(jnp.float32)
    size_x, size_y, size_z = right_side.shape
    block_cells = size_x * size_y * size_z
    layer = lax.broadcasted_iota(jnp.int32, right_side.shape, 2)
    fluid = (layer < extents[0, 0, 0]).astype(jnp.float32)
    fluid_mid = pool_max(fluid)
    cond_mid = pool_sum(conductance) / 8.0
    cond_padded = with_halo(cond_mid, (("gx", 0), ("gy", 1), (GZ, 2)), 1)
    coarse_level = make_level(cond_padded, fluid_mid, 4.0)
    fine_padded = with_halo(conductance, (("gx", 0), ("gy", 1), (GZ, 2)), 1)
    fine_level = make_level(fine_padded, fluid, 1.0)
    levels = [fine_level, coarse_level]
    index_x = lax.axis_index("gx")
    index_y = lax.axis_index("gy")
    index_z = lax.axis_index(GZ)
    count_x = lax.axis_size("gx")
    count_y = lax.axis_size("gy")
    count_z = lax.axis_size(GZ)
    offsets = jnp.arange(3, dtype=jnp.int32) - 1
    near_x = jnp.clip(index_x + offsets, 0, count_x - 1)
    near_y = jnp.clip(index_y + offsets, 0, count_y - 1)
    near_z = jnp.clip(index_z + offsets, 0, count_z - 1)
    near_flat = (near_x[:, None, None] * count_y + near_y[None, :, None]) * count_z + near_z[
        None, None, :
    ]

    def precondition(resid):
        second = cycle(resid, levels)
        padded = with_halo(second, (("gx", 0), ("gy", 1), (GZ, 2)), 1)
        smoothed = second + OMEGA * fine_level[3] * (
            resid - fluid * face_terms(padded, fine_level[0])
        )
        block_mean = jnp.sum(resid) / block_cells
        local_product = jnp.sum(resid * smoothed)
        means, products = (
            gathered_by_axis(block_mean.reshape(1), (("gx", "gy"), ("gz_0", "gz_1")), 0),
            gathered_by_axis(local_product.reshape(1), (("gx", "gy"), ("gz_0", "gz_1")), 0),
        )
        product = jnp.sum(products)
        coarse = jax.scipy.linalg.cho_solve((factor, True), means)
        table = coarse[near_flat]
        precond = smoothed + fluid * table[1, 1, 1]
        inner_value = product + block_cells * jnp.sum(means * coarse)
        precond_wide = None
        return (precond_wide, precond, inner_value)

    resid = fluid * right_side
    solution = jnp.zeros_like(resid)
    precond_wide, precond, inner_now = precondition(resid)
    direction = precond
    for step in range(ITERS):
        padded = with_halo(direction, (("gx", 0), ("gy", 1), (GZ, 2)), 1)
        image = fluid * face_terms(padded, fine_level[0])
        alpha = inner_now / by_axis(jnp.sum(direction * image), (("gx", "gy"), ("gz_0", "gz_1")))
        solution = solution + alpha * direction
        resid = resid - alpha * image
        if step + 1 < ITERS:
            precond_wide, precond, inner_next = precondition(resid)
            ratio = inner_next / inner_now
            direction = precond + ratio * direction
            inner_now = inner_next
    return (solution, resid)


def solution(mesh):
    split = Mesh(
        mesh.devices.reshape(mesh.shape["gx"], mesh.shape["gy"], 8, 2), ("gx", "gy", "gz_0", "gz_1")
    )
    in_specs = (P("gx", "gy", GZ), P("gx", "gy", GZ), P("gx", "gy", GZ), P())
    out_specs = (P("gx", "gy", GZ), P("gx", "gy", GZ))
    return jax.shard_map(
        on_device, mesh=split, in_specs=in_specs, out_specs=out_specs, check_vma=False
    )
```

profile of v0, /device:TPU:6, one launch (start us, length us, event | category | flops | bytes accessed | tf_op | source)
XLA Modules:
  0.0 431.7 jit_solution(4136253935926898240)
XLA Ops:
  13.3 6.3 %reshape.190 = f32[4,2,8,2,64,2]{5,4,3,2,1,0:T(8,128)} reshape(f32[8,16,128]{2,1,0:T(8,128)} %param.7) | data formatting | bytes 131072 | tf_op jit(solution)/shard_map/reshape | solution.py:96
  23.2 8.1 %while.4 = (s32[]{:T(128)}, f32[512,512]{1,0:T(8,128)S(1)}, s32[4,2]{0,1:T(2,128)S(1)}, f32[4,128,128]{2,1,0:T(8,128)S(1)}, s32[]{:T(128)}) while((s32[]{:T(128)}, f32[512,512]{1,0:T(8,128)S(1)}, s32[4,2]{0,1:T(2,128)S(1)}, f32[4,128,128]{2,1,0:T(8,128)S(1)}, s32[]{:T(128)}) %tuple.66), condition=%wide.while_cond, body=%wide.while_body.sunk | while | flops 2 | bytes 131189 | solution.py:169
  32.7 4.5 %collective-permute-start.9 = (f32[4,1,64]{2,1,0:T(1,128)S(1)}, f32[4,1,64]{2,1,0:T(1,128)S(1)}, u32[]{:S(2)}, u32[]{:S(2)}) collective-permute-start(f32[4,1,64]{2,1,0:T(1,128)S(1)} %get-tuple-element.93), channel_id=1, source_target_pairs={{0,16},{16,32},{32,48},{48,64},{64,80},{80,96},{96,112},{1,17},{17... | collective-permute-start | bytes 3080 | tf_op jit(solution)/shard_map/ppermute | solution.py:22
  38.8 4.5 %collective-permute-start.15 = (f32[8,1,128]{2,1,0:T(1,128)S(1)}, f32[8,1,128]{2,1,0:T(1,128)S(1)}, u32[]{:S(2)}, u32[]{:S(2)}) collective-permute-start(f32[8,1,128]{2,1,0:T(1,128)S(1)} %get-tuple-element.83), channel_id=1, source_target_pairs={{0,16},{16,32},{32,48},{48,64},{64,80},{80,96},{96,112},{1,17},{17... | collective-permute-start | bytes 12296 | tf_op jit(solution)/shard_map/ppermute | solution.py:22
  46.0 5.2 %collective-permute-start.12 = (f32[1,16,128]{2,1,0:T(8,128)S(1)}, f32[1,16,128]{2,1,0:T(8,128)S(1)}, u32[]{:S(2)}, u32[]{:S(2)}) collective-permute-start(f32[1,16,128]{2,1,0:T(8,128)S(1)} %get-tuple-element.82), channel_id=1, source_target_pairs={{128,0},{256,128},{384,256},{129,1},{257,129},{385,257},{130,2},{2... | collective-permute-start | bytes 24584 | tf_op jit(solution)/shard_map/ppermute | solution.py:23
  52.6 5.1 %collective-permute-start.17 = (f32[8,16,1]{2,1,0:T(8,128)S(1)}, f32[8,16,1]{2,1,0:T(8,128)S(1)}, u32[]{:S(2)}, u32[]{:S(2)}) collective-permute-start(f32[8,16,1]{2,1,0:T(8,128)S(1)} %get-tuple-element.80), channel_id=1, source_target_pairs={{0,1},{1,2},{2,3},{3,4},{4,5},{5,6},{6,7},{7,8},{8,9},{9,10},{10,1... | collective-permute-start | bytes 1544 | tf_op jit(solution)/shard_map/ppermute | solution.py:22
  59.1 4.5 %collective-permute-start.6 = (f32[1,8,64]{2,1,0:T(8,128)S(1)}, f32[1,8,64]{2,1,0:T(8,128)S(1)}, u32[]{:S(2)}, u32[]{:S(2)}) collective-permute-start(f32[1,8,64]{2,1,0:T(8,128)S(1)} %get-tuple-element.96), channel_id=1, source_target_pairs={{128,0},{256,128},{384,256},{129,1},{257,129},{385,257},{130,2},{2... | collective-permute-start | bytes 6152 | tf_op jit(solution)/shard_map/ppermute | solution.py:23
  65.0 5.1 %collective-permute-start.11 = (f32[4,8,1]{2,1,0:T(8,128)S(1)}, f32[4,8,1]{2,1,0:T(8,128)S(1)}, u32[]{:S(2)}, u32[]{:S(2)}) collective-permute-start(f32[4,8,1]{2,1,0:T(8,128)S(1)} %get-tuple-element.92), channel_id=1, source_target_pairs={{0,1},{1,2},{2,3},{3,4},{4,5},{5,6},{6,7},{7,8},{8,9},{9,10},{10,1... | collective-permute-start | bytes 392 | tf_op jit(solution)/shard_map/ppermute | solution.py:22
  70.3 5.5 %reshape.191 = f32[4,2,8,2,64,2]{5,4,3,2,1,0:T(8,128)} reshape(f32[8,16,128]{2,1,0:T(8,128)S(1)} %fusion.144) | data formatting | bytes 131072 | tf_op jit(solution)/shard_map/reshape | solution.py:96
  92.4 4.5 %collective-permute-start.18 = (f32[1,16,128]{2,1,0:T(8,128)S(1)}, f32[1,16,128]{2,1,0:T(8,128)S(1)}, u32[]{:S(2)}, u32[]{:S(2)}) collective-permute-start(f32[1,16,128]{2,1,0:T(8,128)S(1)} %get-tuple-element.78), channel_id=1, source_target_pairs={{128,0},{256,128},{384,256},{129,1},{257,129},{385,257},{130,2},{2... | collective-permute-start | bytes 24584 | tf_op jit(solution)/shard_map/ppermute | solution.py:23
  104.7 16.8 %all-to-all-start.2 = ((f32[32,1,1]{2,1,0:T(1,128)}), f32[32,1,1]{2,1,0:T(1,128)S(1)}, u32[]{:S(2)}, u32[]{:S(2)}) async-start(f32[32,1,1]{2,1,0:T(1,128)} %broadcast_in_dim.57), calls=%async_computation.2 | async-start | bytes 32768 | tf_op jit(solution)/shard_map/all_to_all | solution.py:36
  121.6 7.7 %all-to-all-done.2 = f32[32,1,1]{2,1,0:T(1,128)S(1)} async-done(((f32[32,1,1]{2,1,0:T(1,128)}), f32[32,1,1]{2,1,0:T(1,128)S(1)}, u32[]{:S(2)}, u32[]{:S(2)}) %all-to-all-start.2) | async-done | bytes 160 | tf_op jit(solution)/shard_map/all_to_all | solution.py:36
  130.2 17.3 %all-to-all-start.3 = ((f32[16,32,1]{1,2,0:T(1,128)}), f32[16,32,1]{1,2,0:T(1,128)S(1)}, u32[]{:S(2)}, u32[]{:S(2)}) async-start(f32[16,32,1]{1,2,0:T(1,128)} %broadcast_in_dim.58), calls=%async_computation.3 | async-start | bytes 16384 | tf_op jit(solution)/shard_map/all_to_all | solution.py:36
  147.5 39.3 %custom-call.6 = f32[4,128,128]{1,2,0:T(8,128)S(1)} custom-call(f32[4,128,128]{2,1,0:T(8,128)S(1)} %get-tuple-element.17), custom_call_target="InvertDiagBlocksLowerTriangular" | custom-call | tf_op jit(solution)/shard_map/jit(_cho_solve)/triangular_solve | solution.py:169
  197.4 4.5 %collective-permute-start.24 = (f32[1,16,128]{2,1,0:T(8,128)S(1)}, f32[1,16,128]{2,1,0:T(8,128)S(1)}, u32[]{:S(2)}, u32[]{:S(2)}) collective-permute-start(f32[1,16,128]{2,1,0:T(8,128)S(1)} %get-tuple-element.72), channel_id=1, source_target_pairs={{128,0},{256,128},{384,256},{129,1},{257,129},{385,257},{130,2},{2... | collective-permute-start | bytes 24584 | tf_op jit(solution)/shard_map/ppermute | solution.py:23
  207.7 8.1 %all-to-all-start = ((f32[32,1,1]{2,1,0:T(1,128)}), f32[32,1,1]{2,1,0:T(1,128)S(1)}, u32[]{:S(2)}, u32[]{:S(2)}) async-start(f32[32,1,1]{2,1,0:T(1,128)} %broadcast_in_dim.55), calls=%async_computation | async-start | bytes 32768 | tf_op jit(solution)/shard_map/all_to_all | solution.py:36
  216.7 7.0 %all-to-all-done = f32[32,1,1]{2,1,0:T(1,128)S(1)} async-done(((f32[32,1,1]{2,1,0:T(1,128)}), f32[32,1,1]{2,1,0:T(1,128)S(1)}, u32[]{:S(2)}, u32[]{:S(2)}) %all-to-all-start) | async-done | bytes 160 | tf_op jit(solution)/shard_map/all_to_all | solution.py:36
  224.9 7.2 %all-to-all-start.4 = ((f32[16,1,1]{2,1,0:T(1,128)}), f32[16,1,1]{2,1,0:T(1,128)S(1)}, u32[]{:S(2)}, u32[]{:S(2)}) async-start(f32[16,1,1]{2,1,0:T(1,128)} %broadcast_in_dim.59), calls=%async_computation.4 | async-start | bytes 16384 | tf_op jit(solution)/shard_map/all_to_all | solution.py:36
  232.5 7.2 %all-to-all-done.4 = f32[16,1,1]{2,1,0:T(1,128)S(1)} async-done(((f32[16,1,1]{2,1,0:T(1,128)}), f32[16,1,1]{2,1,0:T(1,128)S(1)}, u32[]{:S(2)}, u32[]{:S(2)}) %all-to-all-start.4) | async-done | bytes 96 | tf_op jit(solution)/shard_map/all_to_all | solution.py:36
  244.5 6.8 %all-to-all-done.1 = f32[16,32,1]{1,2,0:T(1,128)S(1)} async-done(((f32[16,32,1]{1,2,0:T(1,128)}), f32[16,32,1]{1,2,0:T(1,128)S(1)}, u32[]{:S(2)}, u32[]{:S(2)}) %all-to-all-start.1) | async-done | bytes 2080 | tf_op jit(solution)/shard_map/all_to_all | solution.py:36
  252.5 5.7 %all-to-all-start.5 = ((f32[32,1,1]{2,1,0:T(1,128)}), f32[32,1,1]{2,1,0:T(1,128)S(1)}, u32[]{:S(2)}, u32[]{:S(2)}) async-start(f32[32,1,1]{2,1,0:T(1,128)} %broadcast_in_dim.60), calls=%async_computation.5 | async-start | bytes 32768 | tf_op jit(solution)/shard_map/all_to_all | solution.py:36
  261.0 5.1 %all-to-all-done.5 = f32[32,1,1]{2,1,0:T(1,128)S(1)} async-done(((f32[32,1,1]{2,1,0:T(1,128)}), f32[32,1,1]{2,1,0:T(1,128)S(1)}, u32[]{:S(2)}, u32[]{:S(2)}) %all-to-all-start.5) | async-done | bytes 160 | tf_op jit(solution)/shard_map/all_to_all | solution.py:36
  272.6 4.5 %collective-permute-start.30 = (f32[1,16,128]{2,1,0:T(8,128)S(1)}, f32[1,16,128]{2,1,0:T(8,128)S(1)}, u32[]{:S(2)}, u32[]{:S(2)}) collective-permute-start(f32[1,16,128]{2,1,0:T(8,128)S(1)} %get-tuple-element.64), channel_id=1, source_target_pairs={{128,0},{256,128},{384,256},{129,1},{257,129},{385,257},{130,2},{2... | collective-permute-start | bytes 24584 | tf_op jit(solution)/shard_map/ppermute | solution.py:23
  282.6 5.5 %reshape.193 = f32[4,2,8,2,64,2]{5,4,3,2,1,0:T(8,128)} reshape(f32[8,16,128]{2,1,0:T(8,128)S(1)} %fusion.80) | data formatting | bytes 131072 | tf_op jit(solution)/shard_map/reshape | solution.py:96
  297.3 4.5 %collective-permute-start.39 = (f32[8,1,128]{2,1,0:T(1,128)S(1)}, f32[8,1,128]{2,1,0:T(1,128)S(1)}, u32[]{:S(2)}, u32[]{:S(2)}) collective-permute-start(f32[8,1,128]{2,1,0:T(1,128)S(1)} %get-tuple-element.57), channel_id=1, source_target_pairs={{0,16},{16,32},{32,48},{48,64},{64,80},{80,96},{96,112},{1,17},{17... | collective-permute-start | bytes 12296 | tf_op jit(solution)/shard_map/ppermute | solution.py:22
  315.8 17.1 %all_to_all.80 = f32[32,1,1]{2,1,0:T(1,128)S(1)} all-to-all(f32[32,1,1]{2,1,0:T(1,128)S(1)} %broadcast_in_dim.64), channel_id=1, replica_groups=mesh['gx'=4,'gy'=8,'gz_0'=8,'gz_1'=2] {'gx','gy'}, dimensions={0} | all-to-all | bytes 256 | tf_op jit(solution)/shard_map/all_to_all | solution.py:36
  334.2 5.7 %all-to-all-start.6 = ((f32[32,1,1]{2,1,0:T(1,128)}), f32[32,1,1]{2,1,0:T(1,128)S(1)}, u32[]{:S(2)}, u32[]{:S(2)}) async-start(f32[32,1,1]{2,1,0:T(1,128)} %broadcast_in_dim.62), calls=%async_computation.6 | async-start | bytes 32768 | tf_op jit(solution)/shard_map/all_to_all | solution.py:36
  340.3 7.5 %all-to-all-done.6 = f32[32,1,1]{2,1,0:T(1,128)S(1)} async-done(((f32[32,1,1]{2,1,0:T(1,128)}), f32[32,1,1]{2,1,0:T(1,128)S(1)}, u32[]{:S(2)}, u32[]{:S(2)}) %all-to-all-start.6) | async-done | bytes 160 | tf_op jit(solution)/shard_map/all_to_all | solution.py:36
  348.4 9.5 %all-to-all-start.9 = ((f32[16,32,1]{1,2,0:T(1,128)}), f32[16,32,1]{1,2,0:T(1,128)S(1)}, u32[]{:S(2)}, u32[]{:S(2)}) async-start(f32[16,32,1]{1,2,0:T(1,128)} %broadcast_in_dim.65), calls=%async_computation.9 | async-start | bytes 16384 | tf_op jit(solution)/shard_map/all_to_all | solution.py:36
  358.2 7.2 %all-to-all-done.9 = f32[16,32,1]{1,2,0:T(1,128)S(1)} async-done(((f32[16,32,1]{1,2,0:T(1,128)}), f32[16,32,1]{1,2,0:T(1,128)S(1)}, u32[]{:S(2)}, u32[]{:S(2)}) %all-to-all-start.9) | async-done | bytes 2080 | tf_op jit(solution)/shard_map/all_to_all | solution.py:36
  395.4 16.5 %all_to_all.81 = f32[16,1,1]{2,1,0:T(1,128)S(1)} all-to-all(f32[16,1,1]{2,1,0:T(1,128)S(1)} %broadcast_in_dim.66), channel_id=1, replica_groups=mesh['gx'=4,'gy'=8,'gz_0'=8,'gz_1'=2] {'gz_0','gz_1'}, dimensions={0} | all-to-all | bytes 128 | tf_op jit(solution)/shard_map/all_to_all | solution.py:36
  413.2 15.9 %all_to_all.82 = f32[32,1,1]{2,1,0:T(1,128)S(1)} all-to-all(f32[32,1,1]{2,1,0:T(1,128)S(1)} %broadcast_in_dim.67), channel_id=1, replica_groups=mesh['gx'=4,'gy'=8,'gz_0'=8,'gz_1'=2] {'gx','gy'}, dimensions={0} | all-to-all | bytes 256 | tf_op jit(solution)/shard_map/all_to_all | solution.py:36
  (255 shorter events, 151.3 us)
Async XLA Ops:
  1.4 29.9 %collective-permute-start.3 = (f32[8,1,128]{2,1,0:T(1,128)S(1)}, f32[8,1,128]{2,1,0:T(1,128)S(1)}, u32[]{:S(2)}, u32[]{:S(2)}) collective-permute-start(f32[8,1,128]{2,1,0:T(1,128)S(1)} %get-tuple-element.87), channel_id=1, source_target_pairs={{0,16},{16,32},{32,48},{48,64},{64,80},{80,96},{96,112},{1,17},{17... | collective-permute-start | bytes 12296 | tf_op jit(solution)/shard_map/ppermute | solution.py:22
  4.9 27.8 %collective-permute-start.2 = (f32[8,1,128]{2,1,0:T(1,128)S(1)}, f32[8,1,128]{2,1,0:T(1,128)S(1)}, u32[]{:S(2)}, u32[]{:S(2)}) collective-permute-start(f32[8,1,128]{2,1,0:T(1,128)S(1)} %get-tuple-element.88), channel_id=1, source_target_pairs={{16,0},{32,16},{48,32},{64,48},{80,64},{96,80},{112,96},{17,1},{33... | collective-permute-start | bytes 12296 | tf_op jit(solution)/shard_map/ppermute | solution.py:23
  6.9 31.7 %collective-permute-start = (f32[1,16,128]{2,1,0:T(8,128)S(1)}, f32[1,16,128]{2,1,0:T(8,128)S(1)}, u32[]{:S(2)}, u32[]{:S(2)}) collective-permute-start(f32[1,16,128]{2,1,0:T(8,128)S(1)} %get-tuple-element.89), channel_id=1, source_target_pairs={{128,0},{256,128},{384,256},{129,1},{257,129},{385,257},{130,2},{2... | collective-permute-start | bytes 24584 | tf_op jit(solution)/shard_map/ppermute | solution.py:23
  9.6 27.6 %collective-permute-start.1 = (f32[1,16,128]{2,1,0:T(8,128)S(1)}, f32[1,16,128]{2,1,0:T(8,128)S(1)}, u32[]{:S(2)}, u32[]{:S(2)}) collective-permute-start(f32[1,16,128]{2,1,0:T(8,128)S(1)} %get-tuple-element.90), channel_id=1, source_target_pairs={{0,128},{128,256},{256,384},{1,129},{129,257},{257,385},{2,130},{1... | collective-permute-start | bytes 24584 | tf_op jit(solution)/shard_map/ppermute | solution.py:22
  11.9 26.7 %collective-permute-start.5 = (f32[8,16,1]{2,1,0:T(8,128)S(1)}, f32[8,16,1]{2,1,0:T(8,128)S(1)}, u32[]{:S(2)}, u32[]{:S(2)}) collective-permute-start(f32[8,16,1]{2,1,0:T(8,128)S(1)} %get-tuple-element.85), channel_id=1, source_target_pairs={{0,1},{1,2},{2,3},{3,4},{4,5},{5,6},{6,7},{7,8},{8,9},{9,10},{10,1... | collective-permute-start | bytes 1544 | tf_op jit(solution)/shard_map/ppermute | solution.py:22
  32.7 13.3 %collective-permute-start.9 = (f32[4,1,64]{2,1,0:T(1,128)S(1)}, f32[4,1,64]{2,1,0:T(1,128)S(1)}, u32[]{:S(2)}, u32[]{:S(2)}) collective-permute-start(f32[4,1,64]{2,1,0:T(1,128)S(1)} %get-tuple-element.93), channel_id=1, source_target_pairs={{0,16},{16,32},{32,48},{48,64},{64,80},{80,96},{96,112},{1,17},{17... | collective-permute-start | bytes 3080 | tf_op jit(solution)/shard_map/ppermute | solution.py:22
  37.2 14.0 %collective-permute-start.8 = (f32[4,1,64]{2,1,0:T(1,128)S(1)}, f32[4,1,64]{2,1,0:T(1,128)S(1)}, u32[]{:S(2)}, u32[]{:S(2)}) collective-permute-start(f32[4,1,64]{2,1,0:T(1,128)S(1)} %get-tuple-element.94), channel_id=1, source_target_pairs={{16,0},{32,16},{48,32},{64,48},{80,64},{96,80},{112,96},{17,1},{33... | collective-permute-start | bytes 3080 | tf_op jit(solution)/shard_map/ppermute | solution.py:23
  38.8 13.7 %collective-permute-start.15 = (f32[8,1,128]{2,1,0:T(1,128)S(1)}, f32[8,1,128]{2,1,0:T(1,128)S(1)}, u32[]{:S(2)}, u32[]{:S(2)}) collective-permute-start(f32[8,1,128]{2,1,0:T(1,128)S(1)} %get-tuple-element.83), channel_id=1, source_target_pairs={{0,16},{16,32},{32,48},{48,64},{64,80},{80,96},{96,112},{1,17},{17... | collective-permute-start | bytes 12296 | tf_op jit(solution)/shard_map/ppermute | solution.py:22
  43.4 14.4 %collective-permute-start.14 = (f32[8,1,128]{2,1,0:T(1,128)S(1)}, f32[8,1,128]{2,1,0:T(1,128)S(1)}, u32[]{:S(2)}, u32[]{:S(2)}) collective-permute-start(f32[8,1,128]{2,1,0:T(1,128)S(1)} %get-tuple-element.84), channel_id=1, source_target_pairs={{16,0},{32,16},{48,32},{64,48},{80,64},{96,80},{112,96},{17,1},{33... | collective-permute-start | bytes 12296 | tf_op jit(solution)/shard_map/ppermute | solution.py:23
  44.7 20.3 %collective-permute-start.13 = (f32[1,16,128]{2,1,0:T(8,128)S(1)}, f32[1,16,128]{2,1,0:T(8,128)S(1)}, u32[]{:S(2)}, u32[]{:S(2)}) collective-permute-start(f32[1,16,128]{2,1,0:T(8,128)S(1)} %get-tuple-element.81), channel_id=1, source_target_pairs={{0,128},{128,256},{256,384},{1,129},{129,257},{257,385},{2,130},{1... | collective-permute-start | bytes 24584 | tf_op jit(solution)/shard_map/ppermute | solution.py:22
  46.0 24.1 %collective-permute-start.12 = (f32[1,16,128]{2,1,0:T(8,128)S(1)}, f32[1,16,128]{2,1,0:T(8,128)S(1)}, u32[]{:S(2)}, u32[]{:S(2)}) collective-permute-start(f32[1,16,128]{2,1,0:T(8,128)S(1)} %get-tuple-element.82), channel_id=1, source_target_pairs={{128,0},{256,128},{384,256},{129,1},{257,129},{385,257},{130,2},{2... | collective-permute-start | bytes 24584 | tf_op jit(solution)/shard_map/ppermute | solution.py:23
  57.8 20.6 %collective-permute-start.7 = (f32[1,8,64]{2,1,0:T(8,128)S(1)}, f32[1,8,64]{2,1,0:T(8,128)S(1)}, u32[]{:S(2)}, u32[]{:S(2)}) collective-permute-start(f32[1,8,64]{2,1,0:T(8,128)S(1)} %get-tuple-element.95), channel_id=1, source_target_pairs={{0,128},{128,256},{256,384},{1,129},{129,257},{257,385},{2,130},{1... | collective-permute-start | bytes 6152 | tf_op jit(solution)/shard_map/ppermute | solution.py:22
  59.1 19.3 %collective-permute-start.6 = (f32[1,8,64]{2,1,0:T(8,128)S(1)}, f32[1,8,64]{2,1,0:T(8,128)S(1)}, u32[]{:S(2)}, u32[]{:S(2)}) collective-permute-start(f32[1,8,64]{2,1,0:T(8,128)S(1)} %get-tuple-element.96), channel_id=1, source_target_pairs={{128,0},{256,128},{384,256},{129,1},{257,129},{385,257},{130,2},{2... | collective-permute-start | bytes 6152 | tf_op jit(solution)/shard_map/ppermute | solution.py:23
  63.7 14.7 %collective-permute-start.10 = (f32[4,8,1]{2,1,0:T(8,128)S(1)}, f32[4,8,1]{2,1,0:T(8,128)S(1)}, u32[]{:S(2)}, u32[]{:S(2)}) collective-permute-start(f32[4,8,1]{2,1,0:T(8,128)S(1)} %get-tuple-element.91), channel_id=1, source_target_pairs={{1,0},{2,1},{3,2},{4,3},{5,4},{6,5},{7,6},{8,7},{9,8},{10,9},{11,1... | collective-permute-start | bytes 392 | tf_op jit(solution)/shard_map/ppermute | solution.py:23
  65.0 13.4 %collective-permute-start.11 = (f32[4,8,1]{2,1,0:T(8,128)S(1)}, f32[4,8,1]{2,1,0:T(8,128)S(1)}, u32[]{:S(2)}, u32[]{:S(2)}) collective-permute-start(f32[4,8,1]{2,1,0:T(8,128)S(1)} %get-tuple-element.92), channel_id=1, source_target_pairs={{0,1},{1,2},{2,3},{3,4},{4,5},{5,6},{6,7},{7,8},{8,9},{9,10},{10,1... | collective-permute-start | bytes 392 | tf_op jit(solution)/shard_map/ppermute | solution.py:22
  85.2 13.0 %collective-permute-start.21 = (f32[8,1,128]{2,1,0:T(1,128)S(1)}, f32[8,1,128]{2,1,0:T(1,128)S(1)}, u32[]{:S(2)}, u32[]{:S(2)}) collective-permute-start(f32[8,1,128]{2,1,0:T(1,128)S(1)} %get-tuple-element.75), channel_id=1, source_target_pairs={{0,16},{16,32},{32,48},{48,64},{64,80},{80,96},{96,112},{1,17},{17... | collective-permute-start | bytes 12296 | tf_op jit(solution)/shard_map/ppermute | solution.py:22
  89.8 11.9 %collective-permute-start.20 = (f32[8,1,128]{2,1,0:T(1,128)S(1)}, f32[8,1,128]{2,1,0:T(1,128)S(1)}, u32[]{:S(2)}, u32[]{:S(2)}) collective-permute-start(f32[8,1,128]{2,1,0:T(1,128)S(1)} %get-tuple-element.76), channel_id=1, source_target_pairs={{16,0},{32,16},{48,32},{64,48},{80,64},{96,80},{112,96},{17,1},{33... | collective-permute-start | bytes 12296 | tf_op jit(solution)/shard_map/ppermute | solution.py:23
  104.7 24.7 %all-to-all-start.2 = ((f32[32,1,1]{2,1,0:T(1,128)}), f32[32,1,1]{2,1,0:T(1,128)S(1)}, u32[]{:S(2)}, u32[]{:S(2)}) async-start(f32[32,1,1]{2,1,0:T(1,128)} %broadcast_in_dim.57), calls=%async_computation.2 | async-start | bytes 32768 | tf_op jit(solution)/shard_map/all_to_all | solution.py:36
  130.2 56.6 %all-to-all-start.3 = ((f32[16,32,1]{1,2,0:T(1,128)}), f32[16,32,1]{1,2,0:T(1,128)S(1)}, u32[]{:S(2)}, u32[]{:S(2)}) async-start(f32[16,32,1]{1,2,0:T(1,128)} %broadcast_in_dim.58), calls=%async_computation.3 | async-start | bytes 16384 | tf_op jit(solution)/shard_map/all_to_all | solution.py:36
  194.8 21.0 %collective-permute-start.26 = (f32[8,1,128]{2,1,0:T(1,128)S(1)}, f32[8,1,128]{2,1,0:T(1,128)S(1)}, u32[]{:S(2)}, u32[]{:S(2)}) collective-permute-start(f32[8,1,128]{2,1,0:T(1,128)S(1)} %get-tuple-element.70), channel_id=1, source_target_pairs={{16,0},{32,16},{48,32},{64,48},{80,64},{96,80},{112,96},{17,1},{33... | collective-permute-start | bytes 12296 | tf_op jit(solution)/shard_map/ppermute | solution.py:23
  196.1 19.8 %collective-permute-start.25 = (f32[1,16,128]{2,1,0:T(8,128)S(1)}, f32[1,16,128]{2,1,0:T(8,128)S(1)}, u32[]{:S(2)}, u32[]{:S(2)}) collective-permute-start(f32[1,16,128]{2,1,0:T(8,128)S(1)} %get-tuple-element.71), channel_id=1, source_target_pairs={{0,128},{128,256},{256,384},{1,129},{129,257},{257,385},{2,130},{1... | collective-permute-start | bytes 24584 | tf_op jit(solution)/shard_map/ppermute | solution.py:22
  197.4 18.5 %collective-permute-start.24 = (f32[1,16,128]{2,1,0:T(8,128)S(1)}, f32[1,16,128]{2,1,0:T(8,128)S(1)}, u32[]{:S(2)}, u32[]{:S(2)}) collective-permute-start(f32[1,16,128]{2,1,0:T(8,128)S(1)} %get-tuple-element.72), channel_id=1, source_target_pairs={{128,0},{256,128},{384,256},{129,1},{257,129},{385,257},{130,2},{2... | collective-permute-start | bytes 24584 | tf_op jit(solution)/shard_map/ppermute | solution.py:23
  202.0 13.8 %collective-permute-start.28 = (f32[8,16,1]{2,1,0:T(8,128)S(1)}, f32[8,16,1]{2,1,0:T(8,128)S(1)}, u32[]{:S(2)}, u32[]{:S(2)}) collective-permute-start(f32[8,16,1]{2,1,0:T(8,128)S(1)} %get-tuple-element.67), channel_id=1, source_target_pairs={{1,0},{2,1},{3,2},{4,3},{5,4},{6,5},{7,6},{8,7},{9,8},{10,9},{11,1... | collective-permute-start | bytes 1544 | tf_op jit(solution)/shard_map/ppermute | solution.py:23
  203.3 12.5 %collective-permute-start.29 = (f32[8,16,1]{2,1,0:T(8,128)S(1)}, f32[8,16,1]{2,1,0:T(8,128)S(1)}, u32[]{:S(2)}, u32[]{:S(2)}) collective-permute-start(f32[8,16,1]{2,1,0:T(8,128)S(1)} %get-tuple-element.68), channel_id=1, source_target_pairs={{0,1},{1,2},{2,3},{3,4},{4,5},{5,6},{6,7},{7,8},{8,9},{9,10},{10,1... | collective-permute-start | bytes 1544 | tf_op jit(solution)/shard_map/ppermute | solution.py:22
  207.7 16.0 %all-to-all-start = ((f32[32,1,1]{2,1,0:T(1,128)}), f32[32,1,1]{2,1,0:T(1,128)S(1)}, u32[]{:S(2)}, u32[]{:S(2)}) async-start(f32[32,1,1]{2,1,0:T(1,128)} %broadcast_in_dim.55), calls=%async_computation | async-start | bytes 32768 | tf_op jit(solution)/shard_map/all_to_all | solution.py:36
  224.9 14.7 %all-to-all-start.4 = ((f32[16,1,1]{2,1,0:T(1,128)}), f32[16,1,1]{2,1,0:T(1,128)S(1)}, u32[]{:S(2)}, u32[]{:S(2)}) async-start(f32[16,1,1]{2,1,0:T(1,128)} %broadcast_in_dim.59), calls=%async_computation.4 | async-start | bytes 16384 | tf_op jit(solution)/shard_map/all_to_all | solution.py:36
  252.5 13.5 %all-to-all-start.5 = ((f32[32,1,1]{2,1,0:T(1,128)}), f32[32,1,1]{2,1,0:T(1,128)S(1)}, u32[]{:S(2)}, u32[]{:S(2)}) async-start(f32[32,1,1]{2,1,0:T(1,128)} %broadcast_in_dim.60), calls=%async_computation.5 | async-start | bytes 32768 | tf_op jit(solution)/shard_map/all_to_all | solution.py:36
  270.0 11.6 %collective-permute-start.32 = (f32[8,1,128]{2,1,0:T(1,128)S(1)}, f32[8,1,128]{2,1,0:T(1,128)S(1)}, u32[]{:S(2)}, u32[]{:S(2)}) collective-permute-start(f32[8,1,128]{2,1,0:T(1,128)S(1)} %get-tuple-element.66), channel_id=1, source_target_pairs={{16,0},{32,16},{48,32},{64,48},{80,64},{96,80},{112,96},{17,1},{33... | collective-permute-start | bytes 12296 | tf_op jit(solution)/shard_map/ppermute | solution.py:23
  297.3 13.1 %collective-permute-start.39 = (f32[8,1,128]{2,1,0:T(1,128)S(1)}, f32[8,1,128]{2,1,0:T(1,128)S(1)}, u32[]{:S(2)}, u32[]{:S(2)}) collective-permute-start(f32[8,1,128]{2,1,0:T(1,128)S(1)} %get-tuple-element.57), channel_id=1, source_target_pairs={{0,16},{16,32},{32,48},{48,64},{64,80},{80,96},{96,112},{1,17},{17... | collective-permute-start | bytes 12296 | tf_op jit(solution)/shard_map/ppermute | solution.py:22
  301.9 11.6 %collective-permute-start.38 = (f32[8,1,128]{2,1,0:T(1,128)S(1)}, f32[8,1,128]{2,1,0:T(1,128)S(1)}, u32[]{:S(2)}, u32[]{:S(2)}) collective-permute-start(f32[8,1,128]{2,1,0:T(1,128)S(1)} %get-tuple-element.58), channel_id=1, source_target_pairs={{16,0},{32,16},{48,32},{64,48},{80,64},{96,80},{112,96},{17,1},{33... | collective-permute-start | bytes 12296 | tf_op jit(solution)/shard_map/ppermute | solution.py:23
  334.2 13.5 %all-to-all-start.6 = ((f32[32,1,1]{2,1,0:T(1,128)}), f32[32,1,1]{2,1,0:T(1,128)S(1)}, u32[]{:S(2)}, u32[]{:S(2)}) async-start(f32[32,1,1]{2,1,0:T(1,128)} %broadcast_in_dim.62), calls=%async_computation.6 | async-start | bytes 32768 | tf_op jit(solution)/shard_map/all_to_all | solution.py:36
  348.4 17.0 %all-to-all-start.9 = ((f32[16,32,1]{1,2,0:T(1,128)}), f32[16,32,1]{1,2,0:T(1,128)S(1)}, u32[]{:S(2)}, u32[]{:S(2)}) async-start(f32[16,32,1]{1,2,0:T(1,128)} %broadcast_in_dim.65), calls=%async_computation.9 | async-start | bytes 16384 | tf_op jit(solution)/shard_map/all_to_all | solution.py:36
  (28 other events, 259.6 us)
where the time goes:
time: 435 us; the launch traced here: 432 us
  starting transfers between devices  200 us (46%)
  other arithmetic  60.3 us (14%)
  local copies, waits for them, and re-layouts  54.6 us (13%)
  waiting for transfers between devices  53.4 us (12%)
  blocking collectives  49.6 us (11%)
  between operations  8.06 us (2%)
  matrix products  5.82 us (1%)
    all_to_all x9, starting transfers between devices, from_everyone(): return lax.all_to_all(copies, axis, split_axis=0, concat_axis=0, tiled=True)  77.2 us
    ppermute x24, starting transfers between devices, with_halo(): lax.ppermute(last, axis, up)  66.9 us
    ppermute x24, starting transfers between devices, with_halo(): lax.ppermute(initial, axis, [(b, a) for a, b in up])  55.8 us
    all_to_all x9, waiting for transfers between devices, from_everyone(): return lax.all_to_all(copies, axis, split_axis=0, concat_axis=0, tiled=True)  49.9 us
    all_to_all x3, blocking collectives, from_everyone(): return lax.all_to_all(copies, axis, split_axis=0, concat_axis=0, tiled=True)  49.6 us
    another operation x6, other arithmetic, precondition(): coarse = jax.scipy.linalg.cho_solve((factor, True), means)  39.5 us
    reshape x3, local copies, waits for them, and re-layouts, pool_sum(): field.reshape(first // 2, 2, second // 2, 2, third // 2, 2)  17.4 us
    broadcast_in_dim x12, local copies, waits for them, and re-layouts, from_everyone(): copies = jnp.broadcast_to(x, (lax.axis_size(axis), *x.shape))  9.5 us
  transfers between devices with their start and end apart: 57, of which 12 were waited for; matrix products, arithmetic and copies ran while one was open for 18% of the time, Pallas kernels for 0%

commit v1 on v0

v1 whole, which is shorter than its diff:
```python
import functools

import jax
import jax.numpy as jnp
from jax import lax
from jax.experimental import pallas as pl
from jax.experimental.pallas import tpu as pltpu
from jax.sharding import PartitionSpec as P

MESH = pl.DeviceIdType.MESH
HIGHEST = lax.Precision.HIGHEST
F32 = jnp.float32
NX, NR, NL = 24, 32, 128
SLOTS = [(dx, dy, dz) for dx in (-1, 0, 1) for dy in (-1, 0, 1) for dz in (-1, 0, 1)]
AROUND = [d for d in SLOTS if d != (0, 0, 0)]
PLANAR = [d for d in AROUND if d[2] == 0]
DEEP = [d for d in AROUND if d[2] != 0]


def slot(d):
    return (d[0] + 1) * 9 + (d[1] + 1) * 3 + d[2] + 1


def loop(low, high, unroll, body):
    whole = (high - low) // unroll

    def step(k, carry):
        for u in range(unroll):
            body(low + k * unroll + u)
        return carry

    if whole == 1:
        step(0, 0)
    else:
        lax.fori_loop(0, whole, step, 0)
    for i in range(low + whole * unroll, high):
        body(i)


def kernel(
    dims, rs_ref, c_ref, ext_ref, l_hbm, sol_ref, res_ref,
    R, C, WX, WY, WZ, INV, FI, SEC, V, D0, Q, D1, C1, INV1, F3, F13, FY3,
    KT, LB, YB, G, XT, ZS, ZR, RZ, RY, RX,
    l_sem, e_send, e_recv, x_send, x_recv, z_send, z_recv,
    gz_send, gz_recv, gy_send, gy_recv, gx_send, gx_recv,
):
    n_x, n_y, n_z = dims
    ix, iy, iz = (lax.axis_index(a) for a in ("gx", "gy", "gz"))

    def peer(dx, dy, dz):
        return {
            "gx": lax.rem(ix + dx + n_x, n_x),
            "gy": lax.rem(iy + dy + n_y, n_y),
            "gz": lax.rem(iz + dz + n_z, n_z),
        }

    l_copy = pltpu.make_async_copy(l_hbm, LB, l_sem)
    l_copy.start()

    greet = list(AROUND)
    greet += [(0, 0, o) for o in range(2, n_z - 1)]
    greet += [(0, o, 0) for o in range(2, n_y - 1)]
    greet += [(o, 0, 0) for o in range(2, n_x - 1)]
    barrier = pltpu.get_barrier_semaphore()
    for d in greet:
        pl.semaphore_signal(barrier, inc=1, device_id=peer(*d), device_id_type=MESH)

    lane = lax.broadcasted_iota(jnp.int32, (NR, NL), 1)
    sub = lax.broadcasted_iota(jnp.int32, (NR, NL), 0)
    last_lane, first_lane = lane == NL - 1, lane == 0
    even_z, even_y = lane % 2 == 0, sub % 2 == 0

    def yp(v):
        return pltpu.roll(v, NR - 1, 0)

    def ym(v):
        return pltpu.roll(v, 1, 0)

    def zp(p):
        a, b = pltpu.roll(p[0], NL - 1, 1), pltpu.roll(p[1], NL - 1, 1)
        return jnp.where(last_lane, b, a), jnp.where(last_lane, a, b)

    def zm(p):
        a, b = pltpu.roll(p[0], 1, 1), pltpu.roll(p[1], 1, 1)
        return jnp.where(first_lane, b, a), jnp.where(first_lane, a, b)

    def get(ref, i):
        return ref[i, 0:NR, :], ref[i, NR : 2 * NR, :]

    def put(ref, i, p):
        ref[i, 0:NR, :] = p[0]
        ref[i, NR : 2 * NR, :] = p[1]

    def each(f, *ps):
        return tuple(f(*(p[h] for p in ps)) for h in range(2))

    def pair_y(v):
        return v + jnp.where(even_y, yp(v), ym(v))

    def pair_z(v, op=jnp.add):
        return op(v, jnp.where(even_z, pltpu.roll(v, NL - 1, 1), pltpu.roll(v, 1, 1)))

    def fluid_of(i):
        return get(F3, i // 8)

    def a_plane(of, i, masked=True):
        v, vp, vm = of(i), of(i + 1), of(i - 1)
        wx, wxm, wy, wz = get(WX, i), get(WX, i - 1), get(WY, i), get(WZ, i)
        fy = each(lambda w, a: w * (a - yp(a)), wy, v)
        fz = each(lambda w, a, b: w * (a - b), wz, v, zp(v))
        fzm = zm(fz)
        out = each(
            lambda w, wm, a, ap, am, g, h, hm: w * (a - ap) + wm * (a - am) + (g - ym(g)) + (h - hm),
            wx, wxm, v, vp, vm, fy, fz, fzm,
        )
        if masked:
            out = each(jnp.multiply, fluid_of(i), out)
        return out

    def of(ref):
        return lambda i: get(ref, i)

    extent = jnp.full((1, NL), ext_ref[0, 0, 0].astype(F32))
    XT[13] = extent
    row16 = lax.broadcasted_iota(jnp.int32, (16, NL), 0)
    lane16 = lax.broadcasted_iota(jnp.int32, (16, NL), 1)
    own_fluid = (lane16.astype(F32) < extent).astype(F32)
    total = jnp.zeros((16, NL), F32)
    for i in range(8):
        r = own_fluid * rs_ref[i]
        R[8 + i, 0:16, :] = r
        total = total + r
        C[8 + i, 0:16, :] = c_ref[i]
    r_turned = R[8:16, 0:16, :].reshape(128, 128).T
    c_turned = c_ref[...].reshape(128, 128).T
    for h, at in ((0, 0), (1, 120)):
        ZS[h, 0] = r_turned[at : at + 8]
        ZS[h, 1] = c_turned[at : at + 8]
        ZS[h, 2] = jnp.broadcast_to(extent, (8, NL))

    izlo = lax.rem(iz, 8)

    def message(rows):
        t = jnp.zeros((16, NL), F32)
        for k, row in enumerate(rows):
            t = jnp.where(row16 == k, row, t)
        reduced = jnp.sum(t, axis=1, keepdims=True)
        placed = jnp.where(lane16 == row16 * 8 + izlo, reduced, 0.0)
        return jnp.sum(placed, axis=0, keepdims=True)

    def fold(v):
        return jnp.sum(v, axis=0, keepdims=True)

    pending = []

    def send(src, dst, s_sem, r_sem, to):
        copy = pltpu.make_async_remote_copy(
            src_ref=src, dst_ref=dst, send_sem=s_sem, recv_sem=r_sem,
            device_id=to, device_id_type=MESH,
        )
        copy.start()
        pending.append(copy)
        return copy

    def gather_z(g, row):
        RZ[g, iz] = row
        order = sorted(range(1, n_z), key=lambda o: -min(o, n_z - o))
        return [
            send(RZ.at[g, iz], RZ.at[g, iz], gz_send.at[g, o], gz_recv.at[g, o], peer(0, 0, o))
            for o in order
        ]

    def gather_y(g, before):
        for copy in before:
            copy.wait_recv()
        low, high = RZ[g, 0], RZ[g, 8]
        for k in range(1, 8):
            low, high = low + RZ[g, k], high + RZ[g, 8 + k]
        RY[g, iy, 0:1, :] = low
        RY[g, iy, 1:2, :] = high
        order = sorted(range(1, n_y), key=lambda o: -min(o, n_y - o))
        return [
            send(RY.at[g, iy], RY.at[g, iy], gy_send.at[g, o], gy_recv.at[g, o], peer(0, o, 0))
            for o in order
        ]

    def gather_x(g, before):
        for copy in before:
            copy.wait_recv()
        RX[g, ix] = RY[g]
        return [
            send(RY.at[g], RX.at[g, ix], gx_send.at[g, o], gx_recv.at[g, o], peer(o, 0, 0))
            for o in (2, 1, 3)
        ]

    def gathered(g, before):
        for copy in before:
            copy.wait_recv()
        for a in range(n_x):
            for b in range(n_y):
                at = (a * n_y + b) * 2
                G[at : at + 2, :] = RX[g, a, b]
        return G[...].T

    G[64:128, :] = jnp.zeros((64, NL), F32)
    first_row = message([fold(total)])
    pl.semaphore_wait(barrier, len(greet))

    stage = gather_z(0, first_row)

    incoming = []
    for d in PLANAR:
        dx, dy, _ = d
        to_x = {1: slice(0, 8), -1: slice(16, 24), 0: slice(8, 16)}[dx]
        from_y = {1: slice(8, 16), -1: slice(0, 8), 0: slice(0, 16)}[dy]
        to_y = {1: slice(24, 32), -1: slice(16, 24), 0: slice(0, 16)}[dy]
        back = slot((-dx, -dy, 0))
        k = slot(d)
        for f, ref in enumerate((C, R)):
            incoming.append(send(
                ref.at[8:16, from_y, :], ref.at[to_x, to_y, :],
                e_send.at[f, k], e_recv.at[f, k], peer(*d),
            ))
        incoming.append(send(XT.at[13], XT.at[back], x_send.at[k], x_recv.at[k], peer(*d)))
    for d in DEEP:
        dx, dy, dz = d
        k = slot(d)
        half = (dz + 1) // 2
        incoming.append(send(
            ZS.at[half], ZR.at[1 - half, (1 - dx) * 3 + 1 - dy],
            z_send.at[k], z_recv.at[k], peer(*d),
        ))

    l_copy.wait()
    KT[...] = jnp.zeros_like(KT)
    row = lax.broadcasted_iota(jnp.int32, (128, 128), 0)
    col = lax.broadcasted_iota(jnp.int32, (128, 128), 1)
    eye = row == col
    for b in range(4):
        at = slice(128 * b, 128 * b + 128)
        block = LB[at, at].astype(F32)
        KT[at, at] = jnp.where(eye, 1.0 / jnp.where(eye, block, 1.0), 0.0)

    def dot(a, b, turned=False):
        dims = (((1,), (1 if turned else 0,)), ((), ()))
        return lax.dot_general(a, b, dims, precision=HIGHEST, preferred_element_type=F32)

    def level(k, carry):
        r0, c0 = lax.shift_right_logical(row, k), lax.shift_right_logical(col, k)
        r1, c1 = lax.shift_right_logical(row, k + 1), lax.shift_right_logical(col, k + 1)
        mask = (r1 == c1) & (r0 > c0)
        for b in range(4):
            at = slice(128 * b, 128 * b + 128)
            m = jnp.where(mask, LB[at, at].astype(F32), 0.0)
            kt = KT[at, at]
            KT[at, at] = kt - dot(dot(kt, m, True), kt)
        return carry

    lax.fori_loop(0, 7, level, 0)

    stage = gather_y(0, stage)

    def join(a, b, w):
        up, down = slice(a, a + w), slice(b, b + w)
        l = LB[down, up].astype(F32)
        KT[up, down] = -dot(dot(KT[up, up], l, True), KT[down, down])

    join(0, 128, 128)
    join(256, 384, 128)
    join(0, 256, 256)

    for copy in incoming:
        copy.wait_recv()

    def there(dx, dy, dz):
        ok = None
        for d, i, n in ((dx, ix, n_x), (dy, iy, n_y), (dz, iz, n_z)):
            if d:
                test = i + d >= 0 if d < 0 else i + d < n
                ok = test if ok is None else ok & test
        return jnp.float32(1.0) if ok is None else ok.astype(F32)

    def blockwise(value, dx):
        lower = sub < 16
        upper = sub < 24
        near = [value(dx, dy, 0) for dy in (0, 1, -1)]
        above = [value(dx, dy, 1) for dy in (0, 1, -1)]
        below = [value(dx, dy, -1) for dy in (0, 1, -1)]
        by_y = [jnp.where(lower, a, jnp.where(upper, b, c)) for a, b, c in (near, above, below)]
        return by_y[0], jnp.where(lane < 64, by_y[1], by_y[2])

    def extent_at(dx, dy, dz):
        if dz == 0:
            e = XT[slot((dx, dy, dz))]
        else:
            e = ZR[(dz + 1) // 2, (dx + 1) * 3 + dy + 1, 2, 0:1, :]
        return e * there(dx, dy, dz)

    lane_f = lane.astype(F32)
    for dx in (-1, 0, 1):
        f = each(lambda e: (lane_f < e).astype(F32), blockwise(extent_at, dx))
        put(F3, dx + 1, f)
        put(F13, dx + 1, each(lambda a: pair_z(a, jnp.maximum), f))

    blank = jnp.zeros((104 + 8, NL), F32)
    for dx in (-1, 0, 1):
        to_x = 8 + 8 * dx
        for dy in (-1, 0, 1):
            from_y = {1: 0, -1: 8, 0: 0}[dy]
            to_y = {1: 16, -1: 24, 0: 0}[dy]
            wide = 16 if dy == 0 else 8
            at = (dx + 1) * 3 + dy + 1
            above, below = there(dx, dy, 1), there(dx, dy, -1)
            for f, ref in enumerate((R, C)):
                t = jnp.concatenate([ZR[1, at, f] * above, blank, ZR[0, at, f] * below], axis=0).T
                t = t.reshape(8, 16, NL)
                ref[to_x : to_x + 8, NR + to_y : NR + to_y + wide, :] = t[:, from_y : from_y + wide, :]

    @pl.when(ix == 0)
    def _():
        C[0:8, 0:NR, :] = jnp.zeros((8, NR, NL), F32)

    @pl.when(ix == n_x - 1)
    def _():
        C[16:24, 0:NR, :] = jnp.zeros((8, NR, NL), F32)

    @pl.when(iy == n_y - 1)
    def _():
        C[:, 16:24, :] = jnp.zeros((NX, 8, NL), F32)

    @pl.when(iy == 0)
    def _():
        C[:, 24:32, :] = jnp.zeros((NX, 8, NL), F32)

    def coefficients(i):
        c, cp, cm = get(C, i), get(C, i + 1), get(C, i - 1)
        half = lambda a, b: 0.5 * (a + b)
        wx, wxm = each(half, c, cp), each(half, c, cm)
        wy = each(lambda a: half(a, yp(a)), c)
        wz = each(half, c, zp(c))
        f = fluid_of(i)
        inv = each(
            lambda a, am, b, z, m, g: 0.8 * g / (a + am + b + ym(b) + z + m + 1.0 - g),
            wx, wxm, wy, wz, zm(wz), f,
        )
        put(WX, i, wx)
        put(WY, i, wy)
        put(WZ, i, wz)
        put(INV, i, inv)
        put(FI, i, each(jnp.multiply, inv, get(R, i)))

    loop(1, 23, 2, coefficients)

    def pool(a, b):
        return each(lambda u, v: pair_z(pair_y(u + v)), a, b)

    def coarse_mean(j):
        put(C1, j, each(lambda a: a * 0.125, pool(get(C, 2 * j), get(C, 2 * j + 1))))

    loop(0, 12, 2, coarse_mean)
    near_end, near_start = lane >= NL - 2, lane < 2

    def coarse_inverse(j):
        c = get(C1, j)
        f = get(F13, j // 4)
        u = [pltpu.roll(v, NL - 2, 1) for v in c]
        d = [pltpu.roll(v, 2, 1) for v in c]
        up = (jnp.where(near_end, u[1], u[0]), jnp.where(near_end, u[0], u[1]))
        down = (jnp.where(near_start, d[1], d[0]), jnp.where(near_start, d[0], d[1]))
        put(INV1, j, each(
            lambda a, p, m, g, h, e: 0.8 * e / (
                2.0 * (6.0 * a + p + m + pltpu.roll(a, NR - 2, 0) + pltpu.roll(a, 2, 0) + g + h) + 1.0 - e
            ),
            c, get(C1, j + 1), get(C1, j - 1), up, down, f,
        ))

    loop(1, 11, 2, coarse_inverse)

    def correct(src, low, high):
        def body(j):
            rest = [
                each(jnp.subtract, get(src, i), a_plane(of(FI), i)) for i in (2 * j, 2 * j + 1)
            ]
            below = each(jnp.multiply, get(INV1, j), pool(*rest))
            shift = each(jnp.multiply, get(F3, j // 4), below)
            for i in (2 * j, 2 * j + 1):
                put(SEC, i, each(jnp.add, get(FI, i), shift))

        loop(low, high, 1, body)

    def smooth(src, dst, low, high):
        def body(i):
            put(dst, i, each(
                lambda s, w, r, a: s + w * (r - a),
                get(SEC, i), get(INV, i), get(src, i), a_plane(of(SEC), i),
            ))

        loop(low, high, 2, body)

    stage = gather_x(0, stage)
    correct(R, 1, 11)
    smooth(R, D0, 4, 20)

    def own_sum(p):
        return p[0][0:16]

    def coupling(i, carry):
        e, kz = carry
        f, fn = get(F3, 1), zp(get(F3, 1))
        e = e + own_sum(a_plane(fluid_of, i))
        kz = kz + jnp.where(lane16 == NL - 1, WZ[i, 0:16, :] * f[0][0:16] * fn[0][0:16], 0.0)
        return e, kz

    zero16 = jnp.zeros((16, NL), F32)
    e_part, kz_part = lax.fori_loop(8, 16, coupling, (zero16, zero16))
    kx_part = WX[15, 0:16, :] * F3[1, 0:16, :] * F3[2, 0:16, :]
    ky_part = WY[8, 15:16, :]
    for i in range(9, 16):
        ky_part = ky_part + WY[i, 15:16, :]
    ky_part = ky_part * F3[1, 15:16, :] * F3[1, 16:17, :]

    lane8 = lax.broadcasted_iota(jnp.int32, (8, NL), 1)
    sub8 = lax.broadcasted_iota(jnp.int32, (8, NL), 0)

    def solve(m):
        parts = [[jnp.zeros((8, NL), F32) for _ in range(2)] for _ in range(4)]
        for l in range(64):
            value = jnp.broadcast_to(m[:, l : l + 1], (8, NL))
            for c in range(l // 16, 4):
                parts[c][l % 2] += value * KT[8 * l : 8 * l + 8, NL * c : NL * c + NL]
        t = [jnp.broadcast_to(fold(a + b), (8, NL)) for a, b in parts]
        y = jnp.zeros((8, NL), F32)
        for l in range(64):
            p = None
            for c in range(l // 16, 4):
                q = t[c] * KT[8 * l : 8 * l + 8, NL * c : NL * c + NL]
                p = q if p is None else p + q
            s = jnp.broadcast_to(jnp.sum(p, axis=1, keepdims=True), (8, NL))
            YB[8 * l : 8 * l + 8, :] = s
            y = jnp.where(lane8 == l, s, y)
        return y

    def y_at(dx, dy, dz):
        def held(i, d, n):
            return jnp.clip(i + d, 0, n - 1)

        b = (held(ix, dx, n_x) * n_y + held(iy, dy, n_y)) * n_z + held(iz, dz, n_z)
        return YB[pl.ds(b, 1), :]

    def spread():
        for dx in (-1, 0, 1):
            put(FY3, dx + 1, each(jnp.multiply, get(F3, dx + 1), blockwise(y_at, dx)))

    sums0 = gathered(0, stage)[0:8]
    solve(sums0 * (1.0 / 16384.0))
    spread()

    def add_coarse(i):
        put(D0, i, each(jnp.add, get(D0, i), get(FY3, i // 8)))

    loop(4, 20, 4, add_coarse)

    def first_image(i):
        q = a_plane(of(D0), i)
        put(Q, i, q)
        put(FI, i, each(jnp.multiply, get(INV, i), q))

    loop(5, 19, 2, first_image)
    correct(Q, 3, 9)
    smooth(Q, V, 7, 17)

    def products(i, carry):
        r, d, q, v = (ref[i, 0:16, :] for ref in (R, D0, Q, V))
        w = own_sum(a_plane(of(V), i))
        new = (r * d, d * q, q, r * v, q * v, v * w, w)
        return tuple(a + b for a, b in zip(carry, new))

    parts = lax.fori_loop(8, 16, products, (zero16,) * 7)
    rows = [fold(p) for p in parts]
    rows += [fold(e_part), fold(kx_part), ky_part, fold(kz_part)]
    stage = gather_z(1, message(rows))
    stage = gather_y(1, stage)
    stage = gather_x(1, stage)
    turned = gathered(1, stage)
    rd, dq, q_sum, rv, qv, vw, w_sum, e_all, kx, ky, kz = (
        turned[8 * k : 8 * k + 8] for k in range(11)
    )
    y = solve(q_sum * (1.0 / 16384.0))
    spread()

    def all_sum(v):
        return jnp.sum(jnp.sum(v, axis=0, keepdims=True), axis=1, keepdims=True)

    up = pltpu.roll(y, 7, 0)
    y_z = jnp.where(sub8 == 7, pltpu.roll(up, NL - 1, 1), up)
    y_y = pltpu.roll(y, NL - 2, 1)
    y_x = pltpu.roll(y, NL - 16, 1)
    jump = kx * (y - y_x) ** 2 + ky * (y - y_y) ** 2 + kz * (y - y_z) ** 2
    p1, p2 = all_sum(rd), all_sum(dq)
    p4 = all_sum(rv + sums0 * y)
    p5 = all_sum(qv + q_sum * y)
    p6 = all_sum(vw + 2.0 * y * w_sum + e_all * y * y + jump)
    alpha = p1 / p2
    inner = p1 - alpha * (p4 + p2) + alpha * alpha * p5
    ratio = inner / p1
    grown = 1.0 + ratio
    curve = grown * grown * p2 - 2.0 * grown * alpha * p5 + alpha * alpha * p6
    alpha2 = inner / curve

    def direction(i):
        put(D1, i, each(
            lambda d, v, s: grown * d - alpha * (v + s), get(D0, i), get(V, i), get(FY3, i // 8)
        ))

    loop(7, 17, 2, direction)

    def finish(i):
        d0, d1, r, q = (ref[i, 0:16, :] for ref in (D0, D1, R, Q))
        image = own_sum(a_plane(of(D1), i))
        sol_ref[i - 8] = alpha * d0 + alpha2 * d1
        res_ref[i - 8] = r - alpha * q - alpha2 * image

    loop(8, 16, 2, finish)

    for copy in pending:
        copy.wait_send()


def solution(mesh):
    dims = tuple(mesh.shape[a] for a in ("gx", "gy", "gz"))
    field = pltpu.VMEM((NX, 2 * NR, NL), F32)
    coarse = pltpu.VMEM((NX // 2, 2 * NR, NL), F32)
    three = pltpu.VMEM((3, 2 * NR, NL), F32)
    sems = pltpu.SemaphoreType.DMA

    def on_device(right_side, conductance, extents, coarse_factor):
        shape = jax.ShapeDtypeStruct((8, 16, 128), F32)
        return pl.pallas_call(
            functools.partial(kernel, dims),
            out_shape=(shape, shape),
            in_specs=[
                pl.BlockSpec(memory_space=pltpu.VMEM),
                pl.BlockSpec(memory_space=pltpu.VMEM),
                pl.BlockSpec(memory_space=pltpu.SMEM),
                pl.BlockSpec(memory_space=pl.ANY),
            ],
            out_specs=(
                pl.BlockSpec(memory_space=pltpu.VMEM),
                pl.BlockSpec(memory_space=pltpu.VMEM),
            ),
            scratch_shapes=[
                *([field] * 12), coarse, coarse, three, three, three,
                pltpu.VMEM((512, 512), F32),
                pltpu.VMEM((512, 512), jnp.bfloat16),
                pltpu.VMEM((512, NL), F32),
                pltpu.VMEM((NL, NL), F32),
                pltpu.VMEM((27, 1, NL), F32),
                pltpu.VMEM((2, 3, 8, NL), F32),
                pltpu.VMEM((2, 9, 3, 8, NL), F32),
                pltpu.VMEM((2, 16, 1, NL), F32),
                pltpu.VMEM((2, 8, 2, NL), F32),
                pltpu.VMEM((2, 4, 8, 2, NL), F32),
                sems(()),
                sems((2, 27)), sems((2, 27)),
                sems((27,)), sems((27,)),
                sems((27,)), sems((27,)),
                sems((2, 16)), sems((2, 16)),
                sems((2, 8)), sems((2, 8)),
                sems((2, 4)), sems((2, 4)),
            ],
            compiler_params=pltpu.CompilerParams(collective_id=0, has_side_effects=True),
        )(right_side, conductance, extents, coarse_factor)

    spec = P("gx", "gy", "gz")
    return jax.shard_map(
        on_device, mesh=mesh, in_specs=(spec, spec, spec, P()), out_specs=(spec, spec),
        check_vma=False,
    )
```

time: 435 us -> 64.6 us (0.15)
  starting transfers between devices: 200 us -> 0 us
  other arithmetic: 60.3 us -> 0 us
  Pallas kernels: 0 us -> 60.2 us
  waiting for transfers between devices: 53.4 us -> 0 us
  local copies, waits for them, and re-layouts: 54.6 us -> 2.14 us
  blocking collectives: 49.6 us -> 0 us
  between operations: 8.06 us -> 1.29 us
  matrix products: 5.82 us -> 0 us
    ppermute x48 -> x0, starting transfers between devices: 123 us -> none  [the longest x24 66.9 us: with_halo(): lax.ppermute(last, axis, up)]
    all_to_all x9 -> x0, starting transfers between devices: 77.2 us -> none  [from_everyone(): return lax.all_to_all(copies, axis, split_axis=0, concat_axis=0, tiled=True)]
    pallas_call x0 -> x1, Pallas kernels: none -> 60.2 us  [on_device(): pl.pallas_call(functools.partial(kernel, dims), out_shape=(shape, shape),...]
    all_to_all x9 -> x0, waiting for transfers between devices: 49.9 us -> none  [from_everyone(): return lax.all_to_all(copies, axis, split_axis=0, concat_axis=0, tiled=True)]
    all_to_all x3 -> x0, blocking collectives: 49.6 us -> none  [from_everyone(): return lax.all_to_all(copies, axis, split_axis=0, concat_axis=0, tiled=True)]
    another operation x6 -> x0, other arithmetic: 39.5 us -> none  [precondition(): coarse = jax.scipy.linalg.cho_solve((factor, True), means)]
    reshape x5 -> x0, local copies, waits for them, and re-layouts: 25.4 us -> none  [the longest x3 17.4 us: pool_sum(): field.reshape(first // 2, 2, second // 2, 2, third // 2, 2)]
    reduce_sum x15 -> x0, other arithmetic: 16.1 us -> none  [the longest x3 7.67 us: pool_sum(): field.reshape(first // 2, 2, second // 2, 2, third // 2, 2)]
  transfers between devices with their start and end apart: 57 -> 0, of which waited for: 12 -> 0; matrix products, arithmetic and copies ran while one was open for 18% -> 0% of each run, Pallas kernels for 0% -> 0%
where the time goes in v1:
time: 64.6 us; the launch traced here: 63.6 us
  Pallas kernels  60.2 us (93%)
  local copies, waits for them, and re-layouts  2.14 us (3%)
  between operations  1.29 us (2%)
    pallas_call x1, Pallas kernels, on_device(): pl.pallas_call(functools.partial(kernel, dims), out_shape=(shape, shape),...  60.2 us
    unnamed x4, local copies, waits for them, and re-layouts  2.14 us

profile of v1, /device:TPU:6, one launch (start us, length us, event | category | flops | bytes accessed | tf_op | source)
XLA Modules:
  0.0 63.6 jit_solution(13560392260774390463)
XLA Ops:
  1.3 60.2 %shard_map.59 = (f32[8,16,128]{2,1,0:T(8,128)}, f32[8,16,128]{2,1,0:T(8,128)}) custom-call(f32[8,16,128]{2,1,0:T(8,128)} %rs_ref.1, f32[8,16,128]{2,1,0:T(8,128)} %c_ref.1, s32[1,1,1]{2,1,0:T(1,128)S(6)} %copy.8.ext_ref, bf16[512,512]{1,0:T(8,128)(2,1)} %l_hbm.1), custom_call_target="tpu_custom_call" | custom-call | tf_op jit(solution)/shard_map/pallas_call | solution.py:538
  61.5 0.0 copy-start
  61.5 1.5 %copy.9 = f32[8,16,128]{2,1,0:T(8,128)} copy(f32[8,16,128]{2,1,0:T(8,128)} %get-tuple-element.4) | data formatting | bytes 131072
  63.0 0.0 copy-done
  63.0 0.6 copy.10
Async XLA Ops:
  61.5 1.5 %copy-start = (f32[8,16,128]{2,1,0:T(8,128)S(1)}, f32[8,16,128]{2,1,0:T(8,128)}, u32[]{:S(2)}) copy-start(f32[8,16,128]{2,1,0:T(8,128)} %get-tuple-element.5) | copy-start | bytes 196612

commit v2 on v1

--- a/solution.py
+++ b/solution.py
@@ -8,8 +8,7 @@
 from jax.sharding import PartitionSpec as P
 
 MESH = pl.DeviceIdType.MESH
-HIGHEST = lax.Precision.HIGHEST
-F32 = jnp.float32
+F32, BF16 = jnp.float32, jnp.bfloat16
 NX, NR, NL = 24, 32, 128
 SLOTS = [(dx, dy, dz) for dx in (-1, 0, 1) for dy in (-1, 0, 1) for dz in (-1, 0, 1)]
 AROUND = [d for d in SLOTS if d != (0, 0, 0)]
@@ -19,6 +18,32 @@
 
 def slot(d):
     return (d[0] + 1) * 9 + (d[1] + 1) * 3 + d[2] + 1
+
+
+def dot(a, b, turned=False):
+    dims = (((1,), (1 if turned else 0,)), ((), ()))
+    return lax.dot_general(a, b, dims, preferred_element_type=F32)
+
+
+def three(x):
+    a = x.astype(BF16)
+    rest = x - a.astype(F32)
+    b = rest.astype(BF16)
+    return a, b, (rest - b.astype(F32)).astype(BF16)
+
+
+def dot_turned(x, m):
+    n = x.shape[0]
+    p = dot(jnp.concatenate(three(x), axis=0), m, True)
+    return p[0:n] + (p[n : 2 * n] + p[2 * n :])
+
+
+def dot_wide(x, y):
+    n = x.shape[0]
+    (a, b, c), (d, e, f) = three(x), three(y)
+    p = dot(jnp.concatenate([a, b, c], axis=0), d)
+    q = dot(jnp.concatenate([a, b], axis=0), e)
+    return p[0:n] + ((p[n : 2 * n] + q[0:n]) + (p[2 * n :] + q[n:] + dot(a, f)))
 
 
 def loop(low, high, unroll, body):
@@ -40,9 +65,8 @@
 def kernel(
     dims, rs_ref, c_ref, ext_ref, l_hbm, sol_ref, res_ref,
     R, C, WX, WY, WZ, INV, FI, SEC, V, D0, Q, D1, C1, INV1, F3, F13, FY3,
-    KT, LB, YB, G, XT, ZS, ZR, RZ, RY, RX,
-    l_sem, e_send, e_recv, x_send, x_recv, z_send, z_recv,
-    gz_send, gz_recv, gy_send, gy_recv, gx_send, gx_recv,
+    KT, LB, YB, G, XT, ZS, ZR, RZ, RY, RX, MX, MY, MZ,
+    l_sem, send_sem, recv_sem,
 ):
     n_x, n_y, n_z = dims
     ix, iy, iz = (lax.axis_index(a) for a in ("gx", "gy", "gz"))
@@ -131,12 +155,6 @@
         R[8 + i, 0:16, :] = r
         total = total + r
         C[8 + i, 0:16, :] = c_ref[i]
-    r_turned = R[8:16, 0:16, :].reshape(128, 128).T
-    c_turned = c_ref[...].reshape(128, 128).T
-    for h, at in ((0, 0), (1, 120)):
-        ZS[h, 0] = r_turned[at : at + 8]
-        ZS[h, 1] = c_turned[at : at + 8]
-        ZS[h, 2] = jnp.broadcast_to(extent, (8, NL))
 
     izlo = lax.rem(iz, 8)
 
@@ -153,83 +171,78 @@
 
     pending = []
 
-    def send(src, dst, s_sem, r_sem, to):
-        copy = pltpu.make_async_remote_copy(
-            src_ref=src, dst_ref=dst, send_sem=s_sem, recv_sem=r_sem,
+    def send(src, dst, group, to):
+        pltpu.make_async_remote_copy(
+            src_ref=src, dst_ref=dst, send_sem=send_sem.at[group], recv_sem=recv_sem.at[group],
             device_id=to, device_id_type=MESH,
-        )
-        copy.start()
-        pending.append(copy)
-        return copy
-
-    def gather_z(g, row):
-        RZ[g, iz] = row
-        order = sorted(range(1, n_z), key=lambda o: -min(o, n_z - o))
-        return [
-            send(RZ.at[g, iz], RZ.at[g, iz], gz_send.at[g, o], gz_recv.at[g, o], peer(0, 0, o))
-            for o in order
-        ]
-
-    def gather_y(g, before):
-        for copy in before:
-            copy.wait_recv()
-        low, high = RZ[g, 0], RZ[g, 8]
+        ).start()
+
+    def take(sem, all_bytes):
+        pltpu.make_async_copy(all_bytes, all_bytes, sem).wait()
+
+    def arrived(group, all_bytes):
+        take(recv_sem.at[group], all_bytes)
+        pending.append((group, all_bytes))
+
+    def far_first(n):
+        return sorted(range(1, n), key=lambda o: -min(o, n - o))
+
+    def row_stage(group, ref, at, row, n, direction):
+        ref[at] = row
+        for o in far_first(n):
+            send(ref.at[at], ref.at[at], group, peer(*direction(o)))
+
+    def added(ref, n):
+        row = ref[0]
+        for k in range(1, n):
+            row = row + ref[k]
+        return row
+
+    def gather(row):
+        row_stage(3, RZ, iz, row, n_z, lambda o: (0, 0, o))
+        arrived(3, RZ.at[0 : n_z - 1])
+        low, high = RZ[0], RZ[8]
         for k in range(1, 8):
-            low, high = low + RZ[g, k], high + RZ[g, 8 + k]
-        RY[g, iy, 0:1, :] = low
-        RY[g, iy, 1:2, :] = high
-        order = sorted(range(1, n_y), key=lambda o: -min(o, n_y - o))
-        return [
-            send(RY.at[g, iy], RY.at[g, iy], gy_send.at[g, o], gy_recv.at[g, o], peer(0, o, 0))
-            for o in order
-        ]
-
-    def gather_x(g, before):
-        for copy in before:
-            copy.wait_recv()
-        RX[g, ix] = RY[g]
-        return [
-            send(RY.at[g], RX.at[g, ix], gx_send.at[g, o], gx_recv.at[g, o], peer(o, 0, 0))
-            for o in (2, 1, 3)
-        ]
-
-    def gathered(g, before):
-        for copy in before:
-            copy.wait_recv()
+            low, high = low + RZ[k], high + RZ[8 + k]
+        RY[iy, 0:1, :] = low
+        RY[iy, 1:2, :] = high
+        for o in far_first(n_y):
+            send(RY.at[iy], RY.at[iy], 4, peer(0, o, 0))
+        arrived(4, RY.at[0 : n_y - 1])
+        RX[ix] = RY[...]
+        for o in far_first(n_x):
+            send(RY, RX.at[ix], 5, peer(o, 0, 0))
+        arrived(5, RX.at[0 : n_x - 1])
         for a in range(n_x):
             for b in range(n_y):
                 at = (a * n_y + b) * 2
-                G[at : at + 2, :] = RX[g, a, b]
+                G[at : at + 2, :] = RX[a, b]
         return G[...].T
 
-    G[64:128, :] = jnp.zeros((64, NL), F32)
-    first_row = message([fold(total)])
+    column = (ix * n_y + iy) * 2 + iz // 8
+    lane1 = lax.broadcasted_iota(jnp.int32, (1, NL), 1)
+    first_row = jnp.where(lane1 == column, jnp.sum(fold(total), axis=1, keepdims=True), 0.0)
     pl.semaphore_wait(barrier, len(greet))
-
-    stage = gather_z(0, first_row)
-
-    incoming = []
+    row_stage(0, MX, ix, first_row, n_x, lambda o: (o, 0, 0))
+
     for d in PLANAR:
         dx, dy, _ = d
         to_x = {1: slice(0, 8), -1: slice(16, 24), 0: slice(8, 16)}[dx]
         from_y = {1: slice(8, 16), -1: slice(0, 8), 0: slice(0, 16)}[dy]
         to_y = {1: slice(24, 32), -1: slice(16, 24), 0: slice(0, 16)}[dy]
-        back = slot((-dx, -dy, 0))
-        k = slot(d)
-        for f, ref in enumerate((C, R)):
-            incoming.append(send(
-                ref.at[8:16, from_y, :], ref.at[to_x, to_y, :],
-                e_send.at[f, k], e_recv.at[f, k], peer(*d),
-            ))
-        incoming.append(send(XT.at[13], XT.at[back], x_send.at[k], x_recv.at[k], peer(*d)))
+        for group, ref in ((6, C), (7, R)):
+            send(ref.at[8:16, from_y, :], ref.at[to_x, to_y, :], group, peer(*d))
+        send(XT.at[13], XT.at[slot((-dx, -dy, 0))], 8, peer(*d))
+    r_turned = R[8:16, 0:16, :].reshape(128, 128).T
+    c_turned = c_ref[...].reshape(128, 128).T
+    for h, at in ((0, 0), (1, 120)):
+        ZS[h, 0] = r_turned[at : at + 8]
+        ZS[h, 1] = c_turned[at : at + 8]
+        ZS[h, 2] = jnp.broadcast_to(extent, (8, NL))
     for d in DEEP:
         dx, dy, dz = d
-        k = slot(d)
         half = (dz + 1) // 2
-        incoming.append(send(
-            ZS.at[half], ZR.at[1 - half, (1 - dx) * 3 + 1 - dy],
-            z_send.at[k], z_recv.at[k], peer(*d),
-        ))
+        send(ZS.at[half], ZR.at[1 - half, (1 - dx) * 3 + 1 - dy], 9, peer(*d))
 
     l_copy.wait()
     KT[...] = jnp.zeros_like(KT)
@@ -241,36 +254,35 @@
         block = LB[at, at].astype(F32)
         KT[at, at] = jnp.where(eye, 1.0 / jnp.where(eye, block, 1.0), 0.0)
 
-    def dot(a, b, turned=False):
-        dims = (((1,), (1 if turned else 0,)), ((), ()))
-        return lax.dot_general(a, b, dims, precision=HIGHEST, preferred_element_type=F32)
-
-    def level(k, carry):
-        r0, c0 = lax.shift_right_logical(row, k), lax.shift_right_logical(col, k)
-        r1, c1 = lax.shift_right_logical(row, k + 1), lax.shift_right_logical(col, k + 1)
-        mask = (r1 == c1) & (r0 > c0)
+    def level(k):
+        mask = (row // (2 << k) == col // (2 << k)) & (row // (1 << k) > col // (1 << k))
         for b in range(4):
             at = slice(128 * b, 128 * b + 128)
-            m = jnp.where(mask, LB[at, at].astype(F32), 0.0)
+            m = jnp.where(mask, LB[at, at].astype(F32), 0.0).astype(BF16)
             kt = KT[at, at]
-            KT[at, at] = kt - dot(dot(kt, m, True), kt)
-        return carry
-
-    lax.fori_loop(0, 7, level, 0)
-
-    stage = gather_y(0, stage)
+            KT[at, at] = kt - dot_wide(dot_turned(kt, m), kt)
 
     def join(a, b, w):
         up, down = slice(a, a + w), slice(b, b + w)
-        l = LB[down, up].astype(F32)
-        KT[up, down] = -dot(dot(KT[up, up], l, True), KT[down, down])
-
+        KT[up, down] = -dot_wide(dot_turned(KT[up, up], LB[down, up]), KT[down, down])
+
+    for k in range(4):
+        level(k)
+    arrived(0, MX.at[0 : n_x - 1])
+    row_stage(1, MY, iy, added(MX, n_x), n_y, lambda o: (0, o, 0))
+    for k in range(4, 7):
+        level(k)
     join(0, 128, 128)
     join(256, 384, 128)
     join(0, 256, 256)
-
-    for copy in incoming:
-        copy.wait_recv()
+    G[64:128, :] = jnp.zeros((64, NL), F32)
+    arrived(1, MY.at[0 : n_y - 1])
+    row_stage(2, MZ, iz, added(MY, n_y), n_z, lambda o: (0, 0, o))
+
+    arrived(6, C.at[0:10])
+    arrived(7, R.at[0:10])
+    arrived(8, XT.at[0:8])
+    arrived(9, ZR)
 
     def there(dx, dy, dz):
         ok = None
@@ -397,7 +409,6 @@
 
         loop(low, high, 2, body)
 
-    stage = gather_x(0, stage)
     correct(R, 1, 11)
     smooth(R, D0, 4, 20)
 
@@ -451,7 +462,8 @@
         for dx in (-1, 0, 1):
             put(FY3, dx + 1, each(jnp.multiply, get(F3, dx + 1), blockwise(y_at, dx)))
 
-    sums0 = gathered(0, stage)[0:8]
+    arrived(2, MZ.at[0 : n_z - 1])
+    sums0 = jnp.concatenate([MZ[k] + MZ[k + 8] for k in range(8)], axis=0)
     solve(sums0 * (1.0 / 16384.0))
     spread()
 
@@ -478,10 +490,7 @@
     parts = lax.fori_loop(8, 16, products, (zero16,) * 7)
     rows = [fold(p) for p in parts]
     rows += [fold(e_part), fold(kx_part), ky_part, fold(kz_part)]
-    stage = gather_z(1, message(rows))
-    stage = gather_y(1, stage)
-    stage = gather_x(1, stage)
-    turned = gathered(1, stage)
+    turned = gather(message(rows))
     rd, dq, q_sum, rv, qv, vw, w_sum, e_all, kx, ky, kz = (
         turned[8 * k : 8 * k + 8] for k in range(11)
     )
@@ -522,8 +531,8 @@
 
     loop(8, 16, 2, finish)
 
-    for copy in pending:
-        copy.wait_send()
+    for group, all_bytes in pending:
+        take(send_sem.at[group], all_bytes)
 
 
 def solution(mesh):
@@ -557,16 +566,14 @@
                 pltpu.VMEM((27, 1, NL), F32),
                 pltpu.VMEM((2, 3, 8, NL), F32),
                 pltpu.VMEM((2, 9, 3, 8, NL), F32),
-                pltpu.VMEM((2, 16, 1, NL), F32),
-                pltpu.VMEM((2, 8, 2, NL), F32),
-                pltpu.VMEM((2, 4, 8, 2, NL), F32),
+                pltpu.VMEM((16, 1, NL), F32),
+                pltpu.VMEM((8, 2, NL), F32),
+                pltpu.VMEM((4, 8, 2, NL), F32),
+                pltpu.VMEM((4, 1, NL), F32),
+                pltpu.VMEM((8, 1, NL), F32),
+                pltpu.VMEM((16, 1, NL), F32),
                 sems(()),
-                sems((2, 27)), sems((2, 27)),
-                sems((27,)), sems((27,)),
-                sems((27,)), sems((27,)),
-                sems((2, 16)), sems((2, 16)),
-                sems((2, 8)), sems((2, 8)),
-                sems((2, 4)), sems((2, 4)),
+                sems((10,)), sems((10,)),
             ],
             compiler_params=pltpu.CompilerParams(collective_id=0, has_side_effects=True),
         )(right_side, conductance, extents, coarse_factor)

time: 64.6 us -> 56.7 us (0.88); the launches traced: 63.6 us -> 56.4 us
  Pallas kernels: 60.2 us -> 53 us
    pallas_call x1, Pallas kernels: 60.2 us -> 53 us  [on_device(): pl.pallas_call(functools.partial(kernel, dims), out_shape=(shape, shape),...]
where the time goes in v2:
time: 56.7 us; the launch traced here: 56.4 us
  Pallas kernels  53 us (93%)
  local copies, waits for them, and re-layouts  2.14 us (4%)
  between operations  1.29 us (2%)
    pallas_call x1, Pallas kernels, on_device(): pl.pallas_call(functools.partial(kernel, dims), out_shape=(shape, shape),...  53 us
    unnamed x4, local copies, waits for them, and re-layouts  2.14 us

profile of v2, /device:TPU:6, one launch (start us, length us, event | category | flops | bytes accessed | tf_op | source)
XLA Modules:
  0.0 56.4 jit_solution(6932082339360001261)
XLA Ops:
  1.3 53.0 %shard_map.59 = (f32[8,16,128]{2,1,0:T(8,128)}, f32[8,16,128]{2,1,0:T(8,128)}) custom-call(f32[8,16,128]{2,1,0:T(8,128)} %rs_ref.1, f32[8,16,128]{2,1,0:T(8,128)} %c_ref.1, s32[1,1,1]{2,1,0:T(1,128)S(6)} %copy.8.ext_ref, bf16[512,512]{1,0:T(8,128)(2,1)} %l_hbm.1), custom_call_target="tpu_custom_call" | custom-call | tf_op jit(solution)/shard_map/pallas_call | solution.py:547
  54.3 0.0 copy-start
  54.3 1.5 %copy.9 = f32[8,16,128]{2,1,0:T(8,128)} copy(f32[8,16,128]{2,1,0:T(8,128)} %get-tuple-element.4) | data formatting | bytes 131072
  55.8 0.0 copy-done
  55.8 0.6 %copy.10 = f32[8,16,128]{2,1,0:T(8,128)} copy(f32[8,16,128]{2,1,0:T(8,128)S(1)} %copy-done) | data formatting | bytes 131072
Async XLA Ops:
  54.3 1.5 %copy-start = (f32[8,16,128]{2,1,0:T(8,128)S(1)}, f32[8,16,128]{2,1,0:T(8,128)}, u32[]{:S(2)}) copy-start(f32[8,16,128]{2,1,0:T(8,128)} %get-tuple-element.5) | copy-start | bytes 196612

commit v3 on v2

--- a/solution.py
+++ b/solution.py
@@ -10,6 +10,9 @@
 MESH = pl.DeviceIdType.MESH
 F32, BF16 = jnp.float32, jnp.bfloat16
 NX, NR, NL = 24, 32, 128
+ROWS = 80
+UNROLL = 24
+OWN = slice(16, 32)
 SLOTS = [(dx, dy, dz) for dx in (-1, 0, 1) for dy in (-1, 0, 1) for dz in (-1, 0, 1)]
 AROUND = [d for d in SLOTS if d != (0, 0, 0)]
 PLANAR = [d for d in AROUND if d[2] == 0]
@@ -47,17 +50,18 @@
 
 
 def loop(low, high, unroll, body):
-    whole = (high - low) // unroll
+    if unroll >= high - low:
+        for i in range(low, high):
+            body(i)
+        return
 
     def step(k, carry):
         for u in range(unroll):
             body(low + k * unroll + u)
         return carry
 
-    if whole == 1:
-        step(0, 0)
-    else:
-        lax.fori_loop(0, whole, step, 0)
+    whole = (high - low) // unroll
+    lax.fori_loop(0, whole, step, 0)
     for i in range(low + whole * unroll, high):
         body(i)
 
@@ -91,58 +95,59 @@
 
     lane = lax.broadcasted_iota(jnp.int32, (NR, NL), 1)
     sub = lax.broadcasted_iota(jnp.int32, (NR, NL), 0)
-    last_lane, first_lane = lane == NL - 1, lane == 0
     even_z, even_y = lane % 2 == 0, sub % 2 == 0
 
-    def yp(v):
-        return pltpu.roll(v, NR - 1, 0)
-
-    def ym(v):
-        return pltpu.roll(v, 1, 0)
-
-    def zp(p):
-        a, b = pltpu.roll(p[0], NL - 1, 1), pltpu.roll(p[1], NL - 1, 1)
-        return jnp.where(last_lane, b, a), jnp.where(last_lane, a, b)
-
-    def zm(p):
-        a, b = pltpu.roll(p[0], 1, 1), pltpu.roll(p[1], 1, 1)
-        return jnp.where(first_lane, b, a), jnp.where(first_lane, a, b)
-
-    def get(ref, i):
-        return ref[i, 0:NR, :], ref[i, NR : 2 * NR, :]
+    def at_end(n, width):
+        return lane[0:n] >= NL - width
+
+    def at_start(n, width):
+        return lane[0:n] < width
+
+    def zp(p, width=1):
+        a, b = pltpu.roll(p[0], NL - width, 1), pltpu.roll(p[1], NL - width, 1)
+        edge = at_end(p[0].shape[0], width)
+        return jnp.where(edge, b, a), jnp.where(edge, a, b)
+
+    def zm(p, width=1):
+        a, b = pltpu.roll(p[0], width, 1), pltpu.roll(p[1], width, 1)
+        edge = at_start(p[0].shape[0], width)
+        return jnp.where(edge, b, a), jnp.where(edge, a, b)
+
+    def get(ref, i, off=0, own=False):
+        start, n = (16 + off, 16) if own else (8 + off, NR)
+        return ref[i, start : start + n, :], ref[i, start + NR : start + NR + n, :]
 
     def put(ref, i, p):
-        ref[i, 0:NR, :] = p[0]
-        ref[i, NR : 2 * NR, :] = p[1]
+        ref[i, 8 : 8 + NR, :] = p[0]
+        ref[i, 8 + NR : 8 + 2 * NR, :] = p[1]
 
     def each(f, *ps):
         return tuple(f(*(p[h] for p in ps)) for h in range(2))
 
     def pair_y(v):
-        return v + jnp.where(even_y, yp(v), ym(v))
+        return v + jnp.where(even_y, pltpu.roll(v, NR - 1, 0), pltpu.roll(v, 1, 0))
 
     def pair_z(v, op=jnp.add):
         return op(v, jnp.where(even_z, pltpu.roll(v, NL - 1, 1), pltpu.roll(v, 1, 1)))
 
-    def fluid_of(i):
-        return get(F3, i // 8)
-
-    def a_plane(of, i, masked=True):
-        v, vp, vm = of(i), of(i + 1), of(i - 1)
-        wx, wxm, wy, wz = get(WX, i), get(WX, i - 1), get(WY, i), get(WZ, i)
-        fy = each(lambda w, a: w * (a - yp(a)), wy, v)
+    def of(ref):
+        return lambda i, off, own: get(ref, i, off, own)
+
+    def fluid(i, off, own):
+        return get(F3, i // 8, off, own)
+
+    def a_plane(v_of, i, own=False):
+        v, vp, vm = (v_of(i + k, 0, own) for k in (0, 1, -1))
+        up, down = v_of(i, 1, own), v_of(i, -1, own)
+        wx, wxm = get(WX, i, 0, own), get(WX, i - 1, 0, own)
+        wy, wym, wz = get(WY, i, 0, own), get(WY, i, -1, own), get(WZ, i, 0, own)
         fz = each(lambda w, a, b: w * (a - b), wz, v, zp(v))
-        fzm = zm(fz)
-        out = each(
-            lambda w, wm, a, ap, am, g, h, hm: w * (a - ap) + wm * (a - am) + (g - ym(g)) + (h - hm),
-            wx, wxm, v, vp, vm, fy, fz, fzm,
+        return each(
+            lambda f, w, wm, u, um, a, ap, am, ay, aym, h, hm: f * (
+                (w * (a - ap) + wm * (a - am)) + (u * (a - ay) + um * (a - aym)) + (h - hm)
+            ),
+            fluid(i, 0, own), wx, wxm, wy, wym, v, vp, vm, up, down, fz, zm(fz),
         )
-        if masked:
-            out = each(jnp.multiply, fluid_of(i), out)
-        return out
-
-    def of(ref):
-        return lambda i: get(ref, i)
 
     extent = jnp.full((1, NL), ext_ref[0, 0, 0].astype(F32))
     XT[13] = extent
@@ -152,9 +157,9 @@
     total = jnp.zeros((16, NL), F32)
     for i in range(8):
         r = own_fluid * rs_ref[i]
-        R[8 + i, 0:16, :] = r
+        R[8 + i, OWN, :] = r
         total = total + r
-        C[8 + i, 0:16, :] = c_ref[i]
+        C[8 + i, OWN, :] = c_ref[i]
 
     izlo = lax.rem(iz, 8)
 
@@ -228,12 +233,12 @@
     for d in PLANAR:
         dx, dy, _ = d
         to_x = {1: slice(0, 8), -1: slice(16, 24), 0: slice(8, 16)}[dx]
-        from_y = {1: slice(8, 16), -1: slice(0, 8), 0: slice(0, 16)}[dy]
-        to_y = {1: slice(24, 32), -1: slice(16, 24), 0: slice(0, 16)}[dy]
+        from_y = {1: slice(24, 32), -1: slice(16, 24), 0: OWN}[dy]
+        to_y = {1: slice(8, 16), -1: slice(32, 40), 0: OWN}[dy]
         for group, ref in ((6, C), (7, R)):
             send(ref.at[8:16, from_y, :], ref.at[to_x, to_y, :], group, peer(*d))
         send(XT.at[13], XT.at[slot((-dx, -dy, 0))], 8, peer(*d))
-    r_turned = R[8:16, 0:16, :].reshape(128, 128).T
+    r_turned = R[8:16, OWN, :].reshape(128, 128).T
     c_turned = c_ref[...].reshape(128, 128).T
     for h, at in ((0, 0), (1, 120)):
         ZS[h, 0] = r_turned[at : at + 8]
@@ -279,8 +284,8 @@
     arrived(1, MY.at[0 : n_y - 1])
     row_stage(2, MZ, iz, added(MY, n_y), n_z, lambda o: (0, 0, o))
 
-    arrived(6, C.at[0:10])
-    arrived(7, R.at[0:10])
+    arrived(6, C.at[0:8])
+    arrived(7, R.at[0:8])
     arrived(8, XT.at[0:8])
     arrived(9, ZR)
 
@@ -293,12 +298,12 @@
         return jnp.float32(1.0) if ok is None else ok.astype(F32)
 
     def blockwise(value, dx):
-        lower = sub < 16
-        upper = sub < 24
-        near = [value(dx, dy, 0) for dy in (0, 1, -1)]
-        above = [value(dx, dy, 1) for dy in (0, 1, -1)]
-        below = [value(dx, dy, -1) for dy in (0, 1, -1)]
-        by_y = [jnp.where(lower, a, jnp.where(upper, b, c)) for a, b, c in (near, above, below)]
+        lower = sub < 8
+        middle = sub < 24
+        near = [value(dx, dy, 0) for dy in (-1, 0, 1)]
+        above = [value(dx, dy, 1) for dy in (-1, 0, 1)]
+        below = [value(dx, dy, -1) for dy in (-1, 0, 1)]
+        by_y = [jnp.where(lower, a, jnp.where(middle, b, c)) for a, b, c in (near, above, below)]
         return by_y[0], jnp.where(lane < 64, by_y[1], by_y[2])
 
     def extent_at(dx, dy, dz):
@@ -319,41 +324,40 @@
         to_x = 8 + 8 * dx
         for dy in (-1, 0, 1):
             from_y = {1: 0, -1: 8, 0: 0}[dy]
-            to_y = {1: 16, -1: 24, 0: 0}[dy]
+            to_y = 8 + NR + {1: 24, -1: 0, 0: 8}[dy]
             wide = 16 if dy == 0 else 8
             at = (dx + 1) * 3 + dy + 1
             above, below = there(dx, dy, 1), there(dx, dy, -1)
             for f, ref in enumerate((R, C)):
                 t = jnp.concatenate([ZR[1, at, f] * above, blank, ZR[0, at, f] * below], axis=0).T
                 t = t.reshape(8, 16, NL)
-                ref[to_x : to_x + 8, NR + to_y : NR + to_y + wide, :] = t[:, from_y : from_y + wide, :]
+                ref[to_x : to_x + 8, to_y : to_y + wide, :] = t[:, from_y : from_y + wide, :]
 
     @pl.when(ix == 0)
     def _():
-        C[0:8, 0:NR, :] = jnp.zeros((8, NR, NL), F32)
+        C[0:8, 8:40, :] = jnp.zeros((8, NR, NL), F32)
 
     @pl.when(ix == n_x - 1)
     def _():
-        C[16:24, 0:NR, :] = jnp.zeros((8, NR, NL), F32)
+        C[16:24, 8:40, :] = jnp.zeros((8, NR, NL), F32)
 
     @pl.when(iy == n_y - 1)
     def _():
-        C[:, 16:24, :] = jnp.zeros((NX, 8, NL), F32)
+        C[:, 32:40, :] = jnp.zeros((NX, 8, NL), F32)
 
     @pl.when(iy == 0)
     def _():
-        C[:, 24:32, :] = jnp.zeros((NX, 8, NL), F32)
+        C[:, 8:16, :] = jnp.zeros((NX, 8, NL), F32)
 
     def coefficients(i):
         c, cp, cm = get(C, i), get(C, i + 1), get(C, i - 1)
         half = lambda a, b: 0.5 * (a + b)
         wx, wxm = each(half, c, cp), each(half, c, cm)
-        wy = each(lambda a: half(a, yp(a)), c)
-        wz = each(half, c, zp(c))
-        f = fluid_of(i)
+        wy, wym = each(half, c, get(C, i, 1)), each(half, c, get(C, i, -1))
+        wz, wzm = each(half, c, zp(c)), each(half, c, zm(c))
         inv = each(
-            lambda a, am, b, z, m, g: 0.8 * g / (a + am + b + ym(b) + z + m + 1.0 - g),
-            wx, wxm, wy, wz, zm(wz), f,
+            lambda a, am, b, bm, z, m, g: 0.8 * g / ((a + am) + (b + bm) + (z + m) + 1.0 - g),
+            wx, wxm, wy, wym, wz, wzm, fluid(i, 0, False),
         )
         put(WX, i, wx)
         put(WY, i, wy)
@@ -361,7 +365,7 @@
         put(INV, i, inv)
         put(FI, i, each(jnp.multiply, inv, get(R, i)))
 
-    loop(1, 23, 2, coefficients)
+    loop(1, 23, UNROLL, coefficients)
 
     def pool(a, b):
         return each(lambda u, v: pair_z(pair_y(u + v)), a, b)
@@ -369,24 +373,19 @@
     def coarse_mean(j):
         put(C1, j, each(lambda a: a * 0.125, pool(get(C, 2 * j), get(C, 2 * j + 1))))
 
-    loop(0, 12, 2, coarse_mean)
-    near_end, near_start = lane >= NL - 2, lane < 2
+    loop(0, 12, UNROLL, coarse_mean)
 
     def coarse_inverse(j):
         c = get(C1, j)
-        f = get(F13, j // 4)
-        u = [pltpu.roll(v, NL - 2, 1) for v in c]
-        d = [pltpu.roll(v, 2, 1) for v in c]
-        up = (jnp.where(near_end, u[1], u[0]), jnp.where(near_end, u[0], u[1]))
-        down = (jnp.where(near_start, d[1], d[0]), jnp.where(near_start, d[0], d[1]))
         put(INV1, j, each(
-            lambda a, p, m, g, h, e: 0.8 * e / (
-                2.0 * (6.0 * a + p + m + pltpu.roll(a, NR - 2, 0) + pltpu.roll(a, 2, 0) + g + h) + 1.0 - e
+            lambda a, p, m, u, d, g, h, e: 0.8 * e / (
+                2.0 * (6.0 * a + (p + m) + (u + d) + (g + h)) + 1.0 - e
             ),
-            c, get(C1, j + 1), get(C1, j - 1), up, down, f,
+            c, get(C1, j + 1), get(C1, j - 1), get(C1, j, 2), get(C1, j, -2), zp(c, 2), zm(c, 2),
+            get(F13, j // 4),
         ))
 
-    loop(1, 11, 2, coarse_inverse)
+    loop(1, 11, UNROLL, coarse_inverse)
 
     def correct(src, low, high):
         def body(j):
@@ -398,7 +397,7 @@
             for i in (2 * j, 2 * j + 1):
                 put(SEC, i, each(jnp.add, get(FI, i), shift))
 
-        loop(low, high, 1, body)
+        loop(low, high, UNROLL, body)
 
     def smooth(src, dst, low, high):
         def body(i):
@@ -407,28 +406,23 @@
                 get(SEC, i), get(INV, i), get(src, i), a_plane(of(SEC), i),
             ))
 
-        loop(low, high, 2, body)
+        loop(low, high, UNROLL, body)
 
     correct(R, 1, 11)
     smooth(R, D0, 4, 20)
 
-    def own_sum(p):
-        return p[0][0:16]
-
-    def coupling(i, carry):
-        e, kz = carry
-        f, fn = get(F3, 1), zp(get(F3, 1))
-        e = e + own_sum(a_plane(fluid_of, i))
-        kz = kz + jnp.where(lane16 == NL - 1, WZ[i, 0:16, :] * f[0][0:16] * fn[0][0:16], 0.0)
-        return e, kz
-
-    zero16 = jnp.zeros((16, NL), F32)
-    e_part, kz_part = lax.fori_loop(8, 16, coupling, (zero16, zero16))
-    kx_part = WX[15, 0:16, :] * F3[1, 0:16, :] * F3[2, 0:16, :]
-    ky_part = WY[8, 15:16, :]
+    f_own = get(F3, 1, 0, True)
+    fn_own = zp(f_own)
+    e_part = kz_part = jnp.zeros((16, NL), F32)
+    for i in range(8, 16):
+        e_part = e_part + a_plane(fluid, i, True)[0]
+        kz_part = kz_part + WZ[i, OWN, :]
+    kz_part = jnp.where(lane16 == NL - 1, kz_part * f_own[0] * fn_own[0], 0.0)
+    kx_part = WX[15, OWN, :] * F3[1, OWN, :] * F3[2, OWN, :]
+    ky_part = WY[8, 31:32, :]
     for i in range(9, 16):
-        ky_part = ky_part + WY[i, 15:16, :]
-    ky_part = ky_part * F3[1, 15:16, :] * F3[1, 16:17, :]
+        ky_part = ky_part + WY[i, 31:32, :]
+    ky_part = ky_part * F3[1, 31:32, :] * F3[1, 32:33, :]
 
     lane8 = lax.broadcasted_iota(jnp.int32, (8, NL), 1)
     sub8 = lax.broadcasted_iota(jnp.int32, (8, NL), 0)
@@ -470,24 +464,24 @@
     def add_coarse(i):
         put(D0, i, each(jnp.add, get(D0, i), get(FY3, i // 8)))
 
-    loop(4, 20, 4, add_coarse)
+    loop(4, 20, UNROLL, add_coarse)
 
     def first_image(i):
         q = a_plane(of(D0), i)
         put(Q, i, q)
         put(FI, i, each(jnp.multiply, get(INV, i), q))
 
-    loop(5, 19, 2, first_image)
+    loop(5, 19, UNROLL, first_image)
     correct(Q, 3, 9)
     smooth(Q, V, 7, 17)
 
-    def products(i, carry):
-        r, d, q, v = (ref[i, 0:16, :] for ref in (R, D0, Q, V))
-        w = own_sum(a_plane(of(V), i))
+    parts = [None] * 7
+    for i in range(8, 16):
+        r, d, q, v = (ref[i, OWN, :] for ref in (R, D0, Q, V))
+        w = a_plane(of(V), i, True)[0]
         new = (r * d, d * q, q, r * v, q * v, v * w, w)
-        return tuple(a + b for a, b in zip(carry, new))
-
-    parts = lax.fori_loop(8, 16, products, (zero16,) * 7)
+        parts = [b if a is None else a + b for a, b in zip(parts, new)]
+
     rows = [fold(p) for p in parts]
     rows += [fold(e_part), fold(kx_part), ky_part, fold(kz_part)]
     turned = gather(message(rows))
@@ -521,25 +515,23 @@
             lambda d, v, s: grown * d - alpha * (v + s), get(D0, i), get(V, i), get(FY3, i // 8)
         ))
 
-    loop(7, 17, 2, direction)
-
-    def finish(i):
-        d0, d1, r, q = (ref[i, 0:16, :] for ref in (D0, D1, R, Q))
-        image = own_sum(a_plane(of(D1), i))
+    loop(7, 17, UNROLL, direction)
+
+    for i in range(8, 16):
+        d0, d1, r, q = (ref[i, OWN, :] for ref in (D0, D1, R, Q))
+        image = a_plane(of(D1), i, True)[0]
         sol_ref[i - 8] = alpha * d0 + alpha2 * d1
         res_ref[i - 8] = r - alpha * q - alpha2 * image
 
-    loop(8, 16, 2, finish)
-
     for group, all_bytes in pending:
         take(send_sem.at[group], all_bytes)
 
 
 def solution(mesh):
     dims = tuple(mesh.shape[a] for a in ("gx", "gy", "gz"))
-    field = pltpu.VMEM((NX, 2 * NR, NL), F32)
-    coarse = pltpu.VMEM((NX // 2, 2 * NR, NL), F32)
-    three = pltpu.VMEM((3, 2 * NR, NL), F32)
+    field = pltpu.VMEM((NX, ROWS, NL), F32)
+    coarse = pltpu.VMEM((NX // 2, ROWS, NL), F32)
+    three = pltpu.VMEM((3, ROWS, NL), F32)
     sems = pltpu.SemaphoreType.DMA
 
     def on_device(right_side, conductance, extents, coarse_factor):

time: 56.7 us -> 49.8 us (0.88)
  Pallas kernels: 53 us -> 46.2 us
    pallas_call x1, Pallas kernels: 53 us -> 46.2 us  [on_device(): pl.pallas_call(functools.partial(kernel, dims), out_shape=(shape, shape),...]
where the time goes in v3:
time: 49.8 us; the launch traced here: 49.6 us
  Pallas kernels  46.2 us (93%)
  local copies, waits for them, and re-layouts  2.14 us (4%)
  between operations  1.29 us (3%)
    pallas_call x1, Pallas kernels, on_device(): pl.pallas_call(functools.partial(kernel, dims), out_shape=(shape, shape),...  46.2 us
    unnamed x4, local copies, waits for them, and re-layouts  2.14 us

profile of v3, /device:TPU:6, one launch (start us, length us, event | category | flops | bytes accessed | tf_op | source)
XLA Modules:
  0.0 49.6 jit_solution(14180873755464866336)
XLA Ops:
  1.3 46.2 %shard_map.59 = (f32[8,16,128]{2,1,0:T(8,128)}, f32[8,16,128]{2,1,0:T(8,128)}) custom-call(f32[8,16,128]{2,1,0:T(8,128)} %rs_ref.1, f32[8,16,128]{2,1,0:T(8,128)} %c_ref.1, s32[1,1,1]{2,1,0:T(1,128)S(6)} %copy.8.ext_ref, bf16[512,512]{1,0:T(8,128)(2,1)} %l_hbm.1), custom_call_target="tpu_custom_call" | custom-call | tf_op jit(solution)/shard_map/pallas_call | solution.py:539
  47.5 0.0 copy-start
  47.5 1.5 %copy.9 = f32[8,16,128]{2,1,0:T(8,128)} copy(f32[8,16,128]{2,1,0:T(8,128)} %get-tuple-element.4) | data formatting | bytes 131072
  49.0 0.0 copy-done
  49.0 0.6 %copy.10 = f32[8,16,128]{2,1,0:T(8,128)} copy(f32[8,16,128]{2,1,0:T(8,128)S(1)} %copy-done) | data formatting | bytes 131072
Async XLA Ops:
  47.5 1.5 %copy-start = (f32[8,16,128]{2,1,0:T(8,128)S(1)}, f32[8,16,128]{2,1,0:T(8,128)}, u32[]{:S(2)}) copy-start(f32[8,16,128]{2,1,0:T(8,128)} %get-tuple-element.5) | copy-start | bytes 196612

commit v4 on v3

--- a/solution.py
+++ b/solution.py
@@ -12,6 +12,7 @@
 NX, NR, NL = 24, 32, 128
 ROWS = 80
 UNROLL = 24
+VMEM_LIMIT = 24 << 20
 OWN = slice(16, 32)
 SLOTS = [(dx, dy, dz) for dx in (-1, 0, 1) for dy in (-1, 0, 1) for dz in (-1, 0, 1)]
 AROUND = [d for d in SLOTS if d != (0, 0, 0)]
@@ -67,10 +68,10 @@
 
 
 def kernel(
-    dims, rs_ref, c_ref, ext_ref, l_hbm, sol_ref, res_ref,
+    dims, rs_hbm, c_hbm, ext_ref, l_hbm, sol_ref, res_ref,
     R, C, WX, WY, WZ, INV, FI, SEC, V, D0, Q, D1, C1, INV1, F3, F13, FY3,
-    KT, LB, YB, G, XT, ZS, ZR, RZ, RY, RX, MX, MY, MZ,
-    l_sem, send_sem, recv_sem,
+    KT, LB, YB, G, XT, ZS, ZR, RZ, RY, RX, MX, MY, MZ, RS,
+    in_sem, send_sem, recv_sem,
 ):
     n_x, n_y, n_z = dims
     ix, iy, iz = (lax.axis_index(a) for a in ("gx", "gy", "gz"))
@@ -81,9 +82,6 @@
             "gy": lax.rem(iy + dy + n_y, n_y),
             "gz": lax.rem(iz + dz + n_z, n_z),
         }
-
-    l_copy = pltpu.make_async_copy(l_hbm, LB, l_sem)
-    l_copy.start()
 
     greet = list(AROUND)
     greet += [(0, 0, o) for o in range(2, n_z - 1)]
@@ -92,6 +90,13 @@
     barrier = pltpu.get_barrier_semaphore()
     for d in greet:
         pl.semaphore_signal(barrier, inc=1, device_id=peer(*d), device_id_type=MESH)
+
+    rs_copy = pltpu.make_async_copy(rs_hbm, RS, in_sem.at[0])
+    c_copy = pltpu.make_async_copy(c_hbm, C.at[8:16, OWN, :], in_sem.at[1])
+    l_copy = pltpu.make_async_copy(l_hbm, LB, in_sem.at[2])
+    rs_copy.start()
+    c_copy.start()
+    l_copy.start()
 
     lane = lax.broadcasted_iota(jnp.int32, (NR, NL), 1)
     sub = lax.broadcasted_iota(jnp.int32, (NR, NL), 0)
@@ -155,11 +160,11 @@
     lane16 = lax.broadcasted_iota(jnp.int32, (16, NL), 1)
     own_fluid = (lane16.astype(F32) < extent).astype(F32)
     total = jnp.zeros((16, NL), F32)
+    rs_copy.wait()
     for i in range(8):
-        r = own_fluid * rs_ref[i]
+        r = own_fluid * RS[i]
         R[8 + i, OWN, :] = r
         total = total + r
-        C[8 + i, OWN, :] = c_ref[i]
 
     izlo = lax.rem(iz, 8)
 
@@ -227,6 +232,7 @@
     column = (ix * n_y + iy) * 2 + iz // 8
     lane1 = lax.broadcasted_iota(jnp.int32, (1, NL), 1)
     first_row = jnp.where(lane1 == column, jnp.sum(fold(total), axis=1, keepdims=True), 0.0)
+    c_copy.wait()
     pl.semaphore_wait(barrier, len(greet))
     row_stage(0, MX, ix, first_row, n_x, lambda o: (o, 0, 0))
 
@@ -239,7 +245,7 @@
             send(ref.at[8:16, from_y, :], ref.at[to_x, to_y, :], group, peer(*d))
         send(XT.at[13], XT.at[slot((-dx, -dy, 0))], 8, peer(*d))
     r_turned = R[8:16, OWN, :].reshape(128, 128).T
-    c_turned = c_ref[...].reshape(128, 128).T
+    c_turned = C[8:16, OWN, :].reshape(128, 128).T
     for h, at in ((0, 0), (1, 120)):
         ZS[h, 0] = r_turned[at : at + 8]
         ZS[h, 1] = c_turned[at : at + 8]
@@ -274,15 +280,16 @@
     for k in range(4):
         level(k)
     arrived(0, MX.at[0 : n_x - 1])
-    row_stage(1, MY, iy, added(MX, n_x), n_y, lambda o: (0, o, 0))
+    row_stage(1, MZ, iz, added(MX, n_x), n_z, lambda o: (0, 0, o))
     for k in range(4, 7):
         level(k)
     join(0, 128, 128)
     join(256, 384, 128)
     join(0, 256, 256)
     G[64:128, :] = jnp.zeros((64, NL), F32)
-    arrived(1, MY.at[0 : n_y - 1])
-    row_stage(2, MZ, iz, added(MY, n_y), n_z, lambda o: (0, 0, o))
+    arrived(1, MZ.at[0 : n_z - 1])
+    tile = jnp.concatenate([MZ[k] + MZ[k + 8] for k in range(8)], axis=0)
+    row_stage(2, MY, iy, tile, n_y, lambda o: (0, o, 0))
 
     arrived(6, C.at[0:8])
     arrived(7, R.at[0:8])
@@ -456,8 +463,8 @@
         for dx in (-1, 0, 1):
             put(FY3, dx + 1, each(jnp.multiply, get(F3, dx + 1), blockwise(y_at, dx)))
 
-    arrived(2, MZ.at[0 : n_z - 1])
-    sums0 = jnp.concatenate([MZ[k] + MZ[k + 8] for k in range(8)], axis=0)
+    arrived(2, MY.at[0 : n_y - 1])
+    sums0 = added(MY, n_y)
     solve(sums0 * (1.0 / 16384.0))
     spread()
 
@@ -534,16 +541,19 @@
     three = pltpu.VMEM((3, ROWS, NL), F32)
     sems = pltpu.SemaphoreType.DMA
 
+    def kept(x):
+        return pltpu.with_memory_space_constraint(x, pltpu.HBM)
+
     def on_device(right_side, conductance, extents, coarse_factor):
         shape = jax.ShapeDtypeStruct((8, 16, 128), F32)
         return pl.pallas_call(
             functools.partial(kernel, dims),
             out_shape=(shape, shape),
             in_specs=[
-                pl.BlockSpec(memory_space=pltpu.VMEM),
-                pl.BlockSpec(memory_space=pltpu.VMEM),
+                pl.BlockSpec(memory_space=pltpu.HBM),
+                pl.BlockSpec(memory_space=pltpu.HBM),
                 pl.BlockSpec(memory_space=pltpu.SMEM),
-                pl.BlockSpec(memory_space=pl.ANY),
+                pl.BlockSpec(memory_space=pltpu.HBM),
             ],
             out_specs=(
                 pl.BlockSpec(memory_space=pltpu.VMEM),
@@ -562,13 +572,16 @@
                 pltpu.VMEM((8, 2, NL), F32),
                 pltpu.VMEM((4, 8, 2, NL), F32),
                 pltpu.VMEM((4, 1, NL), F32),
-                pltpu.VMEM((8, 1, NL), F32),
+                pltpu.VMEM((8, 8, NL), F32),
                 pltpu.VMEM((16, 1, NL), F32),
-                sems(()),
+                pltpu.VMEM((8, 16, NL), F32),
+                sems((3,)),
                 sems((10,)), sems((10,)),
             ],
-            compiler_params=pltpu.CompilerParams(collective_id=0, has_side_effects=True),
-        )(right_side, conductance, extents, coarse_factor)
+            compiler_params=pltpu.CompilerParams(
+                collective_id=0, has_side_effects=True, vmem_limit_bytes=VMEM_LIMIT
+            ),
+        )(kept(right_side), kept(conductance), extents, kept(coarse_factor))
 
     spec = P("gx", "gy", "gz")
     return jax.shard_map(

time: 49.8 us -> 47.5 us (0.954)
  Pallas kernels: 46.2 us -> 44.4 us
  local copies, waits for them, and re-layouts: 2.14 us -> 1.26 us
    pallas_call x1, Pallas kernels: 46.2 us -> 44.4 us  [on_device(): pl.pallas_call(functools.partial(kernel, dims), out_shape=(shape, shape),...]
    unnamed x4 -> x2, local copies, waits for them, and re-layouts: 2.14 us -> 1.26 us
where the time goes in v4:
time: 47.5 us; the launch traced here: 47 us
  Pallas kernels  44.4 us (93%)
  between operations  1.28 us (3%)
  local copies, waits for them, and re-layouts  1.26 us (3%)
    pallas_call x1, Pallas kernels, on_device(): pl.pallas_call(functools.partial(kernel, dims), out_shape=(shape, shape),...  44.4 us
    unnamed x2, local copies, waits for them, and re-layouts  1.26 us

profile of v4, /device:TPU:6, one launch (start us, length us, event | category | flops | bytes accessed | tf_op | source)
XLA Modules:
  0.0 47.0 jit_solution(2062717068181027657)
XLA Ops:
  1.3 44.4 %shard_map.59 = (f32[8,16,128]{2,1,0:T(8,128)S(1)}, f32[8,16,128]{2,1,0:T(8,128)S(1)}) custom-call(f32[8,16,128]{2,1,0:T(8,128)} %rs_hbm.1, f32[8,16,128]{2,1,0:T(8,128)} %c_hbm.1, s32[1,1,1]{2,1,0:T(1,128)S(6)} %copy.8.ext_ref, bf16[512,512]{1,0:T(8,128)(2,1)} %l_hbm.1), custom_call_target="tpu_custom_call" | custom-call | tf_op jit(solution)/shard_map/pallas_call | solution.py:549
  45.7 0.6 %copy.9 = f32[8,16,128]{2,1,0:T(8,128)} copy(f32[8,16,128]{2,1,0:T(8,128)S(1)} %get-tuple-element.4) | data formatting | bytes 131072
  46.3 0.6 %copy.10 = f32[8,16,128]{2,1,0:T(8,128)} copy(f32[8,16,128]{2,1,0:T(8,128)S(1)} %get-tuple-element.5) | data formatting | bytes 131072
